TPU v7x, 32 devices: a whole 2x2x4 slice. The times are simulated.
32 devices in a mesh: row: 8 (over y, x, core), col: 4 (over z).
Axes of the slice: x: 2, y: 2, z: 4, core: 2. Of those that a mesh axis runs over, the one named last changes fastest.
Arguments:
- relief: float32 [3, 2048, 4096], P(None, 'row', 'col'), may hold values from -8 to 8
Outputs:
- level_one: float32 [3, 1024, 2048], P(None, 'row', 'col')
- level_two: float32 [3, 512, 1024], P(None, 'row', 'col')
- level_three: float32 [3, 256, 512], P(None, 'row', 'col')
- level_four: float32 [3, 128, 256], P(None, 'row', 'col')
All inputs are finite; a program needn't handle non-finite values.
Results may differ from a plain program's by a relative error of at most 0.00002.
Values sent between devices are 32-bit elements; how exact they have to be, the bound alone decides.
No kernel may reach another device: no remote copies, remote signals or barrier semaphores. Data moves between devices by JAX's collectives and lax.ppermute only.
A program may use at most 64 MiB of HBM per device.

v0:
```python
import jax
import jax.numpy as jnp
from jax import lax
from jax.sharding import PartitionSpec as P

binomial = (0.0625, 0.25, 0.375, 0.25, 0.0625)
margin = 2


def padded_2(cells, sides, width):
    for axis, dim in sides:
        count = lax.axis_size(axis)
        ends = count - 1
        head = lax.slice_in_dim(cells, 0, width, axis=dim)
        tail = lax.slice_in_dim(cells, cells.shape[dim] - width, cells.shape[dim], axis=dim)
        cells = jnp.concatenate(
            [
                lax.ppermute(tail, axis, [(i, (i + 1) % count) for i in range(ends)]),
                cells,
                lax.ppermute(head, axis, [((i + 1) % count, i) for i in range(ends)]),
            ],
            axis=dim,
        )
    return cells


def decimate(padded, along, extent):
    result = binomial[0] * lax.slice_in_dim(padded, 0, extent - 1, 2, along)
    for offset in range(1, 5):
        result = result + binomial[offset] * lax.slice_in_dim(
            padded, offset, offset + extent - 1, 2, along
        )
    return result


def reflect_edges(padded, along, position, final_index, extent):
    upper = jnp.flip(lax.slice_in_dim(padded, margin + 1, 2 * margin + 1, 1, along), along)
    lower = jnp.flip(lax.slice_in_dim(padded, extent - 1, extent + margin - 1, 1, along), along)
    inside = lax.slice_in_dim(padded, margin, margin + extent, 1, along)
    sent_upper = lax.slice_in_dim(padded, 0, margin, 1, along)
    sent_lower = lax.slice_in_dim(padded, margin + extent, 2 * margin + extent, 1, along)
    upper = jnp.where(position == 0, upper, sent_upper)
    lower = jnp.where(position == final_index, lower, sent_lower)
    return jnp.concatenate([upper, inside, lower], along)


def rows_apart(field):
    extent = field.shape[1]
    padded = padded_2(field, (("row", 1),), 2)
    padded = reflect_edges(padded, 1, lax.axis_index("row"), lax.axis_size("row") - 1, extent)
    return decimate(padded, 1, extent)


def cols_apart(field):
    extent = field.shape[2]
    padded = padded_2(field, (("col", 2),), 2)
    padded = reflect_edges(padded, 2, lax.axis_index("col"), lax.axis_size("col") - 1, extent)
    return decimate(padded, 2, extent)


def level_sharded(field):
    return cols_apart(rows_apart(field))


def local(relief):
    level_one = level_sharded(relief)
    level_two = level_sharded(level_one)
    level_three = level_sharded(level_two)
    level_four = level_sharded(level_three)
    return (level_one, level_two, level_three, level_four)


def solution(mesh):
    placed = (P(None, "row", "col"),)
    return jax.shard_map(
        local,
        mesh=mesh,
        in_specs=placed,
        out_specs=(
            P(None, "row", "col"),
            P(None, "row", "col"),
            P(None, "row", "col"),
            P(None, "row", "col"),
        ),
        check_vma=False,
    )
```

profile of v0, /device:TPU:3, one launch (start us, length us, event | category | flops | bytes accessed | tf_op | source)
XLA Modules:
  0.0 345.2 jit_solution(11087502135156873838)
XLA Ops:
  1.7 3.7 %collective-permute-start = (f32[3,2,1024]{2,1,0:T(2,128)S(1)}, f32[3,2,1024]{2,1,0:T(2,128)S(1)}, u32[]{:S(2)}, u32[]{:S(2)}) collective-permute-start(f32[3,2,1024]{2,1,0:T(2,128)S(1)} %get-tuple-element.4), channel_id=1, source_target_pairs={{0,4},{4,8},{8,12},{12,16},{16,20},{20,24},{24,28},{1,5},{5,9},{9,... | collective-permute-start | bytes 73736 | tf_op jit(solution)/shard_map/ppermute | solution.py:18
  7.3 7.8 %slice.222 = f32[3,128,1024]{2,1,0:T(8,128)} slice(f32[3,256,1024]{2,1,0:T(8,128)} %param.1), slice={[0:3:1], [0:255:2], [0:1024:1]} | slice | bytes 3145728 | tf_op jit(solution)/shard_map/slice | solution.py:30
  15.1 4.2 %slice.223 = f32[3,128,1024]{2,1,0:T(8,128)} slice(f32[3,256,1024]{2,1,0:T(8,128)S(1)} %copy-done), slice={[0:3:1], [1:256:2], [0:1024:1]} | slice | bytes 3145728 | tf_op jit(solution)/shard_map/slice | solution.py:30
  22.3 4.2 %slice.220 = f32[3,128,1024]{2,1,0:T(8,128)} slice(f32[3,260,1024]{2,1,0:T(8,128)S(1)} %pad_maximum_fusion), slice={[0:3:1], [0:255:2], [0:1024:1]} | slice | bytes 3145728 | tf_op jit(solution)/shard_map/slice | solution.py:28
  26.5 4.3 %slice.221 = f32[3,128,1024]{2,1,0:T(8,128)} slice(f32[3,260,1024]{2,1,0:T(8,128)S(1)} %pad_maximum_fusion), slice={[0:3:1], [1:256:2], [0:1024:1]} | slice | bytes 3145728 | tf_op jit(solution)/shard_map/slice | solution.py:30
  30.8 4.3 %slice.224 = f32[3,128,1024]{2,1,0:T(8,128)} slice(f32[3,260,1024]{2,1,0:T(8,128)S(1)} %pad_maximum_fusion), slice={[0:3:1], [4:259:2], [0:1024:1]} | slice | bytes 3145728 | tf_op jit(solution)/shard_map/slice | solution.py:30
  35.1 4.2 %multiply_add_fusion = f32[3,128,1024]{2,1,0:T(8,128)S(1)} fusion(f32[3,128,1024]{2,1,0:T(8,128)} %slice.224, f32[3,128,1024]{2,1,0:T(8,128)} %slice.223, f32[3,128,1024]{2,1,0:T(8,128)} %slice.222, f32[3,128,1024]{2,1,0:T(8,128)} %slice.221, f32[3,128,1024]{2,1,0:T(8,128)} %slice.220), kind=kLoop, calls=%fused_computation.1 | loop fusion | flops 3538944 | bytes 9437184 | tf_op jit(solution)/shard_map/add | solution.py:30
  40.9 35.3 %slice.231 = f32[3,128,512]{2,1,0:T(8,128)} slice(f32[3,128,1024]{2,1,0:T(8,128)S(1)} %multiply_add_fusion), slice={[0:3:1], [0:128:1], [0:1023:2]} | slice | bytes 1572864 | tf_op jit(solution)/shard_map/slice | solution.py:30
  76.2 35.3 %slice.232 = f32[3,128,512]{2,1,0:T(8,128)} slice(f32[3,128,1024]{2,1,0:T(8,128)S(1)} %multiply_add_fusion), slice={[0:3:1], [0:128:1], [1:1024:2]} | slice | bytes 1572864 | tf_op jit(solution)/shard_map/slice | solution.py:30
  111.8 4.2 %collective-permute-start.2 = (f32[3,128,2]{2,1,0:T(8,128)S(1)}, f32[3,128,2]{2,1,0:T(8,128)S(1)}, u32[]{:S(2)}, u32[]{:S(2)}) collective-permute-start(f32[3,128,2]{2,1,0:T(8,128)S(1)} %get-tuple-element.10), channel_id=1, source_target_pairs={{0,1},{1,2},{2,3},{4,5},{5,6},{6,7},{8,9},{9,10},{10,11},{12,13},{... | collective-permute-start | bytes 9224 | tf_op jit(solution)/shard_map/ppermute | solution.py:18
  121.7 35.3 %slice.229 = f32[3,128,512]{2,1,0:T(8,128)} slice(f32[3,128,1028]{2,1,0:T(8,128)S(1)} %concatenate.25), slice={[0:3:1], [0:128:1], [0:1023:2]} | slice | bytes 1572864 | tf_op jit(solution)/shard_map/slice | solution.py:28
  157.0 35.3 %slice.230 = f32[3,128,512]{2,1,0:T(8,128)} slice(f32[3,128,1028]{2,1,0:T(8,128)S(1)} %concatenate.25), slice={[0:3:1], [0:128:1], [1:1024:2]} | slice | bytes 1572864 | tf_op jit(solution)/shard_map/slice | solution.py:30
  192.3 35.4 %slice.233 = f32[3,128,512]{2,1,0:T(8,128)} slice(f32[3,128,1028]{2,1,0:T(8,128)S(1)} %concatenate.25), slice={[0:3:1], [0:128:1], [4:1027:2]} | slice | bytes 1572864 | tf_op jit(solution)/shard_map/slice | solution.py:30
  230.1 5.0 %collective-permute-start.4 = (f32[3,2,512]{2,1,0:T(2,128)S(1)}, f32[3,2,512]{2,1,0:T(2,128)S(1)}, u32[]{:S(2)}, u32[]{:S(2)}) collective-permute-start(f32[3,2,512]{2,1,0:T(2,128)S(1)} %get-tuple-element.12), channel_id=1, source_target_pairs={{0,4},{4,8},{8,12},{12,16},{16,20},{20,24},{24,28},{1,5},{5,9},{9,... | collective-permute-start | bytes 36872 | tf_op jit(solution)/shard_map/ppermute | solution.py:18
  238.0 3.8 %collective-permute-done.5 = f32[3,2,512]{2,1,0:T(2,128)S(1)} collective-permute-done((f32[3,2,512]{2,1,0:T(2,128)S(1)}, f32[3,2,512]{2,1,0:T(2,128)S(1)}, u32[]{:S(2)}, u32[]{:S(2)}) %collective-permute-start.5) | collective-permute-done | bytes 12320 | tf_op jit(solution)/shard_map/ppermute | solution.py:20
  243.4 4.3 %collective-permute-start.6 = (f32[3,64,2]{2,1,0:T(8,128)S(1)}, f32[3,64,2]{2,1,0:T(8,128)S(1)}, u32[]{:S(2)}, u32[]{:S(2)}) collective-permute-start(f32[3,64,2]{2,1,0:T(8,128)S(1)} %get-tuple-element.16), channel_id=1, source_target_pairs={{0,1},{1,2},{2,3},{4,5},{5,6},{6,7},{8,9},{9,10},{10,11},{12,13},{... | collective-permute-start | bytes 4616 | tf_op jit(solution)/shard_map/ppermute | solution.py:18
  247.7 8.9 %slice.249 = f32[3,64,256]{2,1,0:T(8,128)S(1)} slice(f32[3,64,512]{2,1,0:T(8,128)S(1)} %multiply_add_fusion.2), slice={[0:3:1], [0:64:1], [0:511:2]} | slice | bytes 393216 | tf_op jit(solution)/shard_map/slice | solution.py:30
  256.6 8.9 %slice.250 = f32[3,64,256]{2,1,0:T(8,128)S(1)} slice(f32[3,64,512]{2,1,0:T(8,128)S(1)} %multiply_add_fusion.2), slice={[0:3:1], [0:64:1], [1:512:2]} | slice | bytes 393216 | tf_op jit(solution)/shard_map/slice | solution.py:30
  267.4 3.5 %collective-permute-done.7 = f32[3,64,2]{2,1,0:T(8,128)S(1)} collective-permute-done((f32[3,64,2]{2,1,0:T(8,128)S(1)}, f32[3,64,2]{2,1,0:T(8,128)S(1)}, u32[]{:S(2)}, u32[]{:S(2)}) %collective-permute-start.7) | collective-permute-done | bytes 1568 | tf_op jit(solution)/shard_map/ppermute | solution.py:20
  271.2 8.9 %slice.247 = f32[3,64,256]{2,1,0:T(8,128)S(1)} slice(f32[3,64,516]{2,1,0:T(8,128)S(1)} %pad_maximum_fusion.2), slice={[0:3:1], [0:64:1], [0:511:2]} | slice | bytes 393216 | tf_op jit(solution)/shard_map/slice | solution.py:28
  280.1 8.9 %slice.248 = f32[3,64,256]{2,1,0:T(8,128)S(1)} slice(f32[3,64,516]{2,1,0:T(8,128)S(1)} %pad_maximum_fusion.2), slice={[0:3:1], [0:64:1], [1:512:2]} | slice | bytes 393216 | tf_op jit(solution)/shard_map/slice | solution.py:30
  289.0 8.9 %slice.251 = f32[3,64,256]{2,1,0:T(8,128)S(1)} slice(f32[3,64,516]{2,1,0:T(8,128)S(1)} %pad_maximum_fusion.2), slice={[0:3:1], [0:64:1], [4:515:2]} | slice | bytes 393216 | tf_op jit(solution)/shard_map/slice | solution.py:30
  303.7 3.8 %collective-permute-done.9 = f32[3,2,256]{2,1,0:T(2,128)S(1)} collective-permute-done((f32[3,2,256]{2,1,0:T(2,128)S(1)}, f32[3,2,256]{2,1,0:T(2,128)S(1)}, u32[]{:S(2)}, u32[]{:S(2)}) %collective-permute-start.9) | collective-permute-done | bytes 6176 | tf_op jit(solution)/shard_map/ppermute | solution.py:20
  330.1 3.8 %collective-permute-done.13 = f32[3,2,128]{2,1,0:T(2,128)S(1)} collective-permute-done((f32[3,2,128]{2,1,0:T(2,128)S(1)}, f32[3,2,128]{2,1,0:T(2,128)S(1)}, u32[]{:S(2)}, u32[]{:S(2)}) %collective-permute-start.13) | collective-permute-done | bytes 3104 | tf_op jit(solution)/shard_map/ppermute | solution.py:20
  (114 shorter events, 61.4 us)
Async XLA Ops:
  1.7 18.2 %collective-permute-start = (f32[3,2,1024]{2,1,0:T(2,128)S(1)}, f32[3,2,1024]{2,1,0:T(2,128)S(1)}, u32[]{:S(2)}, u32[]{:S(2)}) collective-permute-start(f32[3,2,1024]{2,1,0:T(2,128)S(1)} %get-tuple-element.4), channel_id=1, source_target_pairs={{0,4},{4,8},{8,12},{12,16},{16,20},{20,24},{24,28},{1,5},{5,9},{9,... | collective-permute-start | bytes 73736 | tf_op jit(solution)/shard_map/ppermute | solution.py:18
  5.4 14.5 %collective-permute-start.1 = (f32[3,2,1024]{2,1,0:T(2,128)S(1)}, f32[3,2,1024]{2,1,0:T(2,128)S(1)}, u32[]{:S(2)}, u32[]{:S(2)}) collective-permute-start(f32[3,2,1024]{2,1,0:T(2,128)S(1)} %get-tuple-element.5), channel_id=1, source_target_pairs={{4,0},{8,4},{12,8},{16,12},{20,16},{24,20},{28,24},{5,1},{9,5},{13... | collective-permute-start | bytes 73736 | tf_op jit(solution)/shard_map/ppermute | solution.py:20
  7.3 7.8 %copy-start = (f32[3,256,1024]{2,1,0:T(8,128)S(1)}, f32[3,256,1024]{2,1,0:T(8,128)}, u32[]{:S(2)}) copy-start(f32[3,256,1024]{2,1,0:T(8,128)} %param.1) | copy-start | bytes 9437188
  39.5 76.7 %collective-permute-start.3 = (f32[3,128,2]{2,1,0:T(8,128)S(1)}, f32[3,128,2]{2,1,0:T(8,128)S(1)}, u32[]{:S(2)}, u32[]{:S(2)}) collective-permute-start(f32[3,128,2]{2,1,0:T(8,128)S(1)} %get-tuple-element.8), channel_id=1, source_target_pairs={{1,0},{2,1},{3,2},{5,4},{6,5},{7,6},{9,8},{10,9},{11,10},{13,12},{... | collective-permute-start | bytes 9224 | tf_op jit(solution)/shard_map/ppermute | solution.py:20
  111.8 7.3 %collective-permute-start.2 = (f32[3,128,2]{2,1,0:T(8,128)S(1)}, f32[3,128,2]{2,1,0:T(8,128)S(1)}, u32[]{:S(2)}, u32[]{:S(2)}) collective-permute-start(f32[3,128,2]{2,1,0:T(8,128)S(1)} %get-tuple-element.10), channel_id=1, source_target_pairs={{0,1},{1,2},{2,3},{4,5},{5,6},{6,7},{8,9},{9,10},{10,11},{12,13},{... | collective-permute-start | bytes 9224 | tf_op jit(solution)/shard_map/ppermute | solution.py:18
  157.0 70.7 %copy-start.2 = (f32[3,128,512]{2,1,0:T(8,128)S(1)}, f32[3,128,512]{2,1,0:T(8,128)}, u32[]{:S(2)}) copy-start(f32[3,128,512]{2,1,0:T(8,128)} %slice.231) | copy-start | bytes 2359300
  230.0 11.9 %copy-start.1 = (f32[3,128,512]{2,1,0:T(8,128)}, f32[3,128,512]{2,1,0:T(8,128)S(1)}, u32[]{:S(2)}) copy-start(f32[3,128,512]{2,1,0:T(8,128)S(1)} %multiply_add_fusion.1) | copy-start | bytes 2359300
  230.1 7.9 %collective-permute-start.4 = (f32[3,2,512]{2,1,0:T(2,128)S(1)}, f32[3,2,512]{2,1,0:T(2,128)S(1)}, u32[]{:S(2)}, u32[]{:S(2)}) collective-permute-start(f32[3,2,512]{2,1,0:T(2,128)S(1)} %get-tuple-element.12), channel_id=1, source_target_pairs={{0,4},{4,8},{8,12},{12,16},{16,20},{20,24},{24,28},{1,5},{5,9},{9,... | collective-permute-start | bytes 36872 | tf_op jit(solution)/shard_map/ppermute | solution.py:18
  235.9 5.9 %collective-permute-start.5 = (f32[3,2,512]{2,1,0:T(2,128)S(1)}, f32[3,2,512]{2,1,0:T(2,128)S(1)}, u32[]{:S(2)}, u32[]{:S(2)}) collective-permute-start(f32[3,2,512]{2,1,0:T(2,128)S(1)} %get-tuple-element.13), channel_id=1, source_target_pairs={{4,0},{8,4},{12,8},{16,12},{20,16},{24,20},{28,24},{5,1},{9,5},{13... | collective-permute-start | bytes 36872 | tf_op jit(solution)/shard_map/ppermute | solution.py:20
  243.4 24.0 %collective-permute-start.6 = (f32[3,64,2]{2,1,0:T(8,128)S(1)}, f32[3,64,2]{2,1,0:T(8,128)S(1)}, u32[]{:S(2)}, u32[]{:S(2)}) collective-permute-start(f32[3,64,2]{2,1,0:T(8,128)S(1)} %get-tuple-element.16), channel_id=1, source_target_pairs={{0,1},{1,2},{2,3},{4,5},{5,6},{6,7},{8,9},{9,10},{10,11},{12,13},{... | collective-permute-start | bytes 4616 | tf_op jit(solution)/shard_map/ppermute | solution.py:18
  265.6 5.4 %collective-permute-start.7 = (f32[3,64,2]{2,1,0:T(8,128)S(1)}, f32[3,64,2]{2,1,0:T(8,128)S(1)}, u32[]{:S(2)}, u32[]{:S(2)}) collective-permute-start(f32[3,64,2]{2,1,0:T(8,128)S(1)} %get-tuple-element.17), channel_id=1, source_target_pairs={{1,0},{2,1},{3,2},{5,4},{6,5},{7,6},{9,8},{10,9},{11,10},{13,12},{... | collective-permute-start | bytes 4616 | tf_op jit(solution)/shard_map/ppermute | solution.py:20
  298.0 21.4 %copy-start.3 = (f32[3,64,256]{2,1,0:T(8,128)}, f32[3,64,256]{2,1,0:T(8,128)S(1)}, u32[]{:S(2)}) copy-start(f32[3,64,256]{2,1,0:T(8,128)S(1)} %multiply_add_fusion.3) | copy-start | bytes 589828
  298.0 5.6 %collective-permute-start.8 = (f32[3,2,256]{2,1,0:T(2,128)S(1)}, f32[3,2,256]{2,1,0:T(2,128)S(1)}, u32[]{:S(2)}, u32[]{:S(2)}) collective-permute-start(f32[3,2,256]{2,1,0:T(2,128)S(1)} %get-tuple-element.20), channel_id=1, source_target_pairs={{0,4},{4,8},{8,12},{12,16},{16,20},{20,24},{24,28},{1,5},{5,9},{9,... | collective-permute-start | bytes 18440 | tf_op jit(solution)/shard_map/ppermute | solution.py:18
  301.6 5.8 %collective-permute-start.9 = (f32[3,2,256]{2,1,0:T(2,128)S(1)}, f32[3,2,256]{2,1,0:T(2,128)S(1)}, u32[]{:S(2)}, u32[]{:S(2)}) collective-permute-start(f32[3,2,256]{2,1,0:T(2,128)S(1)} %get-tuple-element.21), channel_id=1, source_target_pairs={{4,0},{8,4},{12,8},{16,12},{20,16},{24,20},{28,24},{5,1},{9,5},{13... | collective-permute-start | bytes 18440 | tf_op jit(solution)/shard_map/ppermute | solution.py:20
  307.8 8.2 %collective-permute-start.10 = (f32[3,32,2]{2,1,0:T(8,128)S(1)}, f32[3,32,2]{2,1,0:T(8,128)S(1)}, u32[]{:S(2)}, u32[]{:S(2)}) collective-permute-start(f32[3,32,2]{2,1,0:T(8,128)S(1)} %get-tuple-element.24), channel_id=1, source_target_pairs={{0,1},{1,2},{2,3},{4,5},{5,6},{6,7},{8,9},{9,10},{10,11},{12,13},{... | collective-permute-start | bytes 2312 | tf_op jit(solution)/shard_map/ppermute | solution.py:18
  314.6 4.8 %collective-permute-start.11 = (f32[3,32,2]{2,1,0:T(8,128)S(1)}, f32[3,32,2]{2,1,0:T(8,128)S(1)}, u32[]{:S(2)}, u32[]{:S(2)}) collective-permute-start(f32[3,32,2]{2,1,0:T(8,128)S(1)} %get-tuple-element.25), channel_id=1, source_target_pairs={{1,0},{2,1},{3,2},{5,4},{6,5},{7,6},{9,8},{10,9},{11,10},{13,12},{... | collective-permute-start | bytes 2312 | tf_op jit(solution)/shard_map/ppermute | solution.py:20
  324.6 20.4 %copy-start.4 = (f32[3,32,128]{2,1,0:T(8,128)}, f32[3,32,128]{2,1,0:T(8,128)S(1)}, u32[]{:S(2)}) copy-start(f32[3,32,128]{2,1,0:T(8,128)S(1)} %multiply_add_fusion.5) | copy-start | bytes 147460
  324.7 5.4 %collective-permute-start.12 = (f32[3,2,128]{2,1,0:T(2,128)S(1)}, f32[3,2,128]{2,1,0:T(2,128)S(1)}, u32[]{:S(2)}, u32[]{:S(2)}) collective-permute-start(f32[3,2,128]{2,1,0:T(2,128)S(1)} %get-tuple-element.28), channel_id=1, source_target_pairs={{0,4},{4,8},{8,12},{12,16},{16,20},{20,24},{24,28},{1,5},{5,9},{9,... | collective-permute-start | bytes 9224 | tf_op jit(solution)/shard_map/ppermute | solution.py:18
  328.1 5.8 %collective-permute-start.13 = (f32[3,2,128]{2,1,0:T(2,128)S(1)}, f32[3,2,128]{2,1,0:T(2,128)S(1)}, u32[]{:S(2)}, u32[]{:S(2)}) collective-permute-start(f32[3,2,128]{2,1,0:T(2,128)S(1)} %get-tuple-element.29), channel_id=1, source_target_pairs={{4,0},{8,4},{12,8},{16,12},{20,16},{24,20},{28,24},{5,1},{9,5},{13... | collective-permute-start | bytes 9224 | tf_op jit(solution)/shard_map/ppermute | solution.py:20
  334.6 5.1 %collective-permute-start.14 = (f32[3,16,2]{2,1,0:T(8,128)S(1)}, f32[3,16,2]{2,1,0:T(8,128)S(1)}, u32[]{:S(2)}, u32[]{:S(2)}) collective-permute-start(f32[3,16,2]{2,1,0:T(8,128)S(1)} %get-tuple-element.32), channel_id=1, source_target_pairs={{0,1},{1,2},{2,3},{4,5},{5,6},{6,7},{8,9},{9,10},{10,11},{12,13},{... | collective-permute-start | bytes 1160 | tf_op jit(solution)/shard_map/ppermute | solution.py:18
  338.3 4.6 %collective-permute-start.15 = (f32[3,16,2]{2,1,0:T(8,128)S(1)}, f32[3,16,2]{2,1,0:T(8,128)S(1)}, u32[]{:S(2)}, u32[]{:S(2)}) collective-permute-start(f32[3,16,2]{2,1,0:T(8,128)S(1)} %get-tuple-element.33), channel_id=1, source_target_pairs={{1,0},{2,1},{3,2},{5,4},{6,5},{7,6},{9,8},{10,9},{11,10},{13,12},{... | collective-permute-start | bytes 1160 | tf_op jit(solution)/shard_map/ppermute | solution.py:20
where the time goes:
time: 352 us; the launch traced here: 345 us
  local copies, waits for them, and re-layouts  264 us (75%)
  starting transfers between devices  43.7 us (12%)
  waiting for transfers between devices  24.4 us (7%)
  other arithmetic  11.3 us (3%)
    slice x32, local copies, waits for them, and re-layouts, decimate(): lax.slice_in_dim(padded, offset, offset + extent - 1, 2, along)  208 us
    slice x8, local copies, waits for them, and re-layouts, decimate(): result = binomial[0] * lax.slice_in_dim(padded, 0, extent - 1, 2, along)  51 us
    ppermute x8, starting transfers between devices, padded_2(): lax.ppermute(tail, axis, [(i, (i + 1) % count) for i in range(ends)])  30.5 us
    ppermute x8, waiting for transfers between devices, padded_2(): lax.ppermute(head, axis, [((i + 1) % count, i) for i in range(ends)])  21.6 us
    ppermute x8, starting transfers between devices, padded_2(): lax.ppermute(head, axis, [((i + 1) % count, i) for i in range(ends)])  13.2 us
    add x8, other arithmetic, decimate(): result + binomial[offset] * lax.slice_in_dim(padded, offset, offset + ext...  7.52 us
  transfers between devices with their start and end apart: 16, of which 7 were waited for; matrix products, arithmetic and copies ran while one was open for 31% of the time, Pallas kernels for 0%

commit v1 on v0

v1 whole, which is shorter than its diff:
```python
import functools

import jax
import jax.numpy as jnp
from jax import lax
from jax.experimental import pallas as pl
from jax.experimental.pallas import tpu as pltpu
from jax.sharding import PartitionSpec as P

F32 = jnp.float32
BF16 = jnp.bfloat16
FAR = 1 << 20
LEVELS = 4
VMEM = pl.BlockSpec(memory_space=pltpu.VMEM)
PAD = 8
TAIL = 24


def lanes_of(cols):
    return (cols + 3 + 127) // 128 * 128


def iota(shape, dim):
    return lax.broadcasted_iota(jnp.int32, shape, dim)


def band(source, target):
    far = jnp.abs(source - 2 * target)
    return jnp.where(far == 0, 0.375, jnp.where(far == 1, 0.25, jnp.where(far == 2, 0.0625, 0.0))).astype(F32)


def block_matrix(first, last):
    source, lane = iota((256, 256), 0), iota((256, 256), 1)
    target = jnp.where(lane <= 128, lane, jnp.where(lane == 255, -1, FAR))
    value = band(source, target)
    if first is not None:
        value += first * jnp.where(source >= 1, band(-source, target), 0.0)
    if last is not None:
        value += last * jnp.where(source == 254, band(source + 2, target), 0.0)
    return value.astype(BF16)


def rim_matrix(first, last):
    source, lane = iota((128, 256), 0), iota((128, 256), 1)
    after = source < 64
    col = jnp.where(after, 512 + source, source - 128)
    own = jnp.where(lane < 2, 256 + lane, jnp.where(lane == 127, -1, FAR))
    other = jnp.where(lane == 128, 0, jnp.where(lane == 255, 255, FAR))
    value = band(col, jnp.where(lane < 128, own, other))
    keep = jnp.where(after, 1.0 - last, 1.0 - first)
    return (value * keep).astype(BF16)


def last_matrix(cols, first, last):
    source, lane = iota((2 * cols, cols), 0), iota((2 * cols, cols), 1)
    half = cols // 2
    col = jnp.where(source < cols + cols // 2, source, source - 2 * cols)
    target = jnp.where(lane < half + 2, lane, jnp.where(lane == cols - 1, -1, FAR))
    value = band(col, target)
    value += first * jnp.where((source >= 1) & (source < cols), band(-source, target), 0.0)
    value += last * jnp.where(source == cols - 2, band(source + 2, target), 0.0)
    keep = jnp.where(col < 0, 1.0 - first, jnp.where(col >= cols, 1.0 - last, 1.0))
    return (value * keep).astype(BF16)


def split_dot(value, matrix):
    high = value.astype(BF16)
    low = (value - high.astype(F32)).astype(BF16)
    return (
        jnp.dot(high, matrix, preferred_element_type=F32)
        + jnp.dot(low, matrix, preferred_element_type=F32)
    )


def columns(tiles, cols, matrices):
    blocks = cols // 256
    rim = len(tiles) > 2 * blocks
    parts = []
    for t in range(blocks):
        index = (1 if t == 0 else 0) + (2 if t == blocks - 1 else 0)
        value = jnp.concatenate(tiles[2 * t:2 * t + 2], 1)
        parts.append(split_dot(value, matrices[index][...]))
    near = iota((tiles[0].shape[0], 128), 1) < 64
    edges = [p[:, 128:] for p in parts]
    if rim:
        around = split_dot(tiles[-1], matrices[4][...])
        edges.append(around[:, 128:])
    else:
        edges.append(jnp.zeros_like(edges[0]))
    out = [
        parts[t][:, :128] + jnp.where(near, edges[t - 1], edges[t + 1])
        for t in range(blocks)
    ]
    outer = jnp.where(near, edges[blocks - 1], edges[0])
    if rim:
        outer = outer + around[:, :128]
    return out + [outer]


def rows(ref, extent):
    half = extent // 2

    def reduced(start, size):
        e = [ref[pl.ds(start + t, size, stride=2), :] for t in range(5)]
        return 0.0625 * (e[0] + e[4]) + 0.25 * (e[1] + e[3]) + 0.375 * e[2]

    main = reduced(PAD - 2, half)
    below = reduced(PAD - 2 + extent, 8)
    above = 0.25 * ref[PAD - 1:PAD, :] + 0.0625 * ref[PAD:PAD + 1, :]
    return jnp.concatenate([main, jnp.where(iota(below.shape, 0) == 7, above, below)], 0)


def close(ref, extent, first, last):
    @pl.when(first)
    def _():
        ref[:, PAD - 2:PAD - 1, :] = ref[:, PAD + 2:PAD + 3, :]
        ref[:, PAD - 1:PAD, :] = ref[:, PAD + 1:PAD + 2, :]

    @pl.when(last)
    def _():
        ref[:, PAD + extent:PAD + extent + 1, :] = ref[:, PAD + extent - 2:PAD + extent - 1, :]


def pyramid_kernel(
    shape, counts, x_hbm, one, two, three, four, rim_a, rim_b, send_e, send_o,
    s0, s1, s2, s3, mats, rim_mat, end_mat, sems,
):
    bands, n, m = shape
    row, col = lax.axis_index("row"), lax.axis_index("col")
    top, bottom = row == 0, row == counts[0] - 1
    copies = [
        [
            pltpu.make_async_copy(
                x_hbm.at[b, :, pl.ds(128 * t, 128)], s0.at[b, t, pl.ds(PAD, n), :], sems.at[b, t]
            )
            for t in range(m // 128)
        ]
        for b in range(bands)
    ]
    for copy in sum(copies, []):
        copy.start()
    left = jnp.where(col == 0, 1.0, 0.0).astype(F32)
    right = jnp.where(col == counts[1] - 1, 1.0, 0.0).astype(F32)
    mats[0] = block_matrix(None, None)
    mats[1] = block_matrix(left, None)
    mats[2] = block_matrix(None, right)
    mats[3] = block_matrix(left, right)
    rim_mat[...] = rim_matrix(left, right)
    end_mat[...] = last_matrix(end_mat.shape[1], left, right)
    matrices = [mats.at[i] for i in range(4)] + [rim_mat]
    fields, outs = [s0, s1, s2, s3], [one, two, three, four]
    for k, ref in enumerate(fields):
        extent = n >> k
        skip = 0 if k == 0 else 8
        if k == 0:
            ref[:, :, 0:PAD, :] = jnp.zeros(ref.shape[:2] + (PAD, 128), F32)
        ref[:, :, PAD + extent + skip:, :] = jnp.zeros(ref.shape[:2] + (TAIL - skip, 128), F32)
    rim_b[...] = jnp.zeros_like(rim_b)
    down = [[jnp.zeros((8, 128), F32)] * (lanes_of(m >> (k + 1)) // 128) for k in range(LEVELS)]
    up = [list(d) for d in down]
    sub = iota((8, 128), 0)
    for k in range(LEVELS):
        extent, cols = n >> k, m >> k
        half = extent // 2
        for b in range(bands):
            if k == 0:
                for copy in copies[b]:
                    copy.wait()
            close(fields[k].at[b], extent, top, bottom)
            tiles = [rows(fields[k].at[b, t], extent) for t in range(fields[k].shape[1])]
            if k < LEVELS - 1:
                tiles = columns(tiles, cols, matrices)
            else:
                tiles = [split_dot(jnp.concatenate(tiles, 1), end_mat[...])]
            for t, tile in enumerate(tiles):
                body, tail = tile[:half], tile[half:]
                if k < LEVELS - 1:
                    after = fields[k + 1]
                    after[b, t, PAD:PAD + half, :] = body
                    after[b, t, 0:PAD, :] = jnp.where(sub == 7, tail, 0.0)
                    after[b, t, PAD + half:PAD + half + 8, :] = jnp.where(sub < 2, tail, 0.0)
                    if t < len(tiles) - 1:
                        outs[k][b, :, 128 * t:128 * t + 128] = body
                moved = pltpu.roll(tail, 2 * b, 0) if b else tail
                down[k][t] = jnp.where((sub >= 2 * b) & (sub < 2 * b + 2), moved, down[k][t])
                up[k][t] = jnp.where(sub == 2 * b, pltpu.roll(tail, 2 * b + 1, 0), up[k][t])
            body = tiles[-1][:half]
            start = sum(n >> j for j in range(2, k + 1))
            if k == LEVELS - 1:
                four[b] = body[:, :cols // 2]
                body = jnp.where(iota(body.shape, 1) < 2, pltpu.roll(body, 128 - cols // 2, 1), body)
            if k == 0:
                rim_a[b] = body
            else:
                rim_b[b, start:start + half, :] = body
    down, up = jnp.concatenate(sum(down, []), 1), jnp.concatenate(sum(up, []), 1)
    even = (row & 1) == 0
    send_e[...] = jnp.where(even, down, up)
    send_o[...] = jnp.where(even, up, down)


def from_rows(got_e, got_o):
    even = (lax.axis_index("row") & 1) == 0
    e, o = got_e[...], got_o[...]
    return jnp.where(even, o, e), jnp.where(even, e, o)


def upper(part, b):
    part = pltpu.roll(part, 8 - 2 * b, 0) if b else part
    return jnp.where(iota(part.shape, 0) < 2, part, 0.0)


def lower(part, b):
    part = pltpu.roll(part, 7 - 2 * b, 0)
    return jnp.where(iota(part.shape, 0) == 7, part, 0.0)


def segments(n):
    out, start = [], 0
    for k in range(2, LEVELS + 1):
        out.append((k, start, n >> k))
        start += n >> k
    return out


def rim_kernel(shape, rim_a, rim_b, got_e, got_o, send_e, send_o, tile_a, tile_b):
    bands, n, m = shape
    above, below = from_rows(got_e, got_o)
    offsets, start = [], 0
    for k in range(1, LEVELS + 1):
        cols = m >> k
        offsets.append(start + (cols if cols >= 128 else 0))
        start += lanes_of(cols)

    def rim_of(part, k):
        part = part[:, offsets[k - 1]:offsets[k - 1] + 128]
        if (m >> k) < 128:
            part = jnp.where(iota(part.shape, 1) < 2, pltpu.roll(part, 128 - (m >> k), 1), part)
        return part

    sub = iota((16, 128), 0)
    to_right, to_left = jnp.zeros((16, 128), F32), jnp.zeros((16, 128), F32)
    for b in range(bands):
        half = n // 2
        tile_a[b] = rim_a[b]
        tile_b[b] = rim_b[b]
        for ref, k, first, size in [(tile_a, 1, 0, half)] + [(tile_b, k, s, z) for k, s, z in segments(n)]:
            ref[b, first:first + 8, :] += upper(rim_of(above, k), b)
            ref[b, first + size - 8:first + size, :] += lower(rim_of(below, k), b)
        a = jnp.transpose(tile_a[b])
        c = jnp.transpose(tile_b[b])
        to_right = jnp.where(sub == 4 * b, a[0:1], to_right)
        to_right = jnp.where(sub == 4 * b + 1, c[0:1], to_right)
        to_right = jnp.where(sub == 4 * b + 2, c[1:2], to_right)
        to_left = jnp.where(sub == 4 * b, a[127:128], to_left)
        to_left = jnp.where(sub == 4 * b + 1, c[127:128], to_left)
    even = (lax.axis_index("col") & 1) == 0
    send_e[...] = jnp.where(even, to_right, to_left)
    send_o[...] = jnp.where(even, to_left, to_right)


def finish_kernel(
    shape, one, two, three, four, row_e, row_o, col_e, col_o,
    out_one, out_two, out_three, out_four, tile_a, tile_b,
):
    bands, n, m = shape
    above, below = from_rows(row_e, row_o)
    even = (lax.axis_index("col") & 1) == 0
    before = jnp.where(even, col_o[...], col_e[...])
    after = jnp.where(even, col_e[...], col_o[...])
    fields, outs = [one, two, three, four], [out_one, out_two, out_three, out_four]
    tile_a[...] = jnp.zeros_like(tile_a)
    tile_b[...] = jnp.zeros_like(tile_b)
    lane = iota((128, 128), 1)
    for b in range(bands):
        tile_a[b, 0:1, :] = before[4 * b:4 * b + 1]
        tile_a[b, 127:128, :] = after[4 * b:4 * b + 1]
        tile_b[b, 0:2, :] = before[4 * b + 1:4 * b + 3]
        tile_b[b, 127:128, :] = after[4 * b + 1:4 * b + 2]
        tile_b[b, 63:64, :] = after[4 * b + 1:4 * b + 2]
        a = jnp.transpose(tile_a[b])
        c = jnp.transpose(tile_b[b])
        start = 0
        for k, first, size in [(1, 0, n // 2)] + segments(n):
            cols = m >> k
            part = (a if k == 1 else c)[first:first + size]
            wide = min(cols, 128)
            spot = lane[:size, :wide]
            part = part[:, :wide]
            low, high = jnp.where(spot < 2, part, 0.0), jnp.where(spot == wide - 1, part, 0.0)
            for t in range(cols // wide):
                at = pl.ds(wide * t, wide)
                value = fields[k - 1][b, :, at]
                if t == 0:
                    value = value + low
                if t == cols // wide - 1:
                    value = value + high
                outs[k - 1][b, :, at] = value
            top = upper(above[:, start:start + cols], b)
            end = lower(below[:, start:start + cols], b)
            outs[k - 1][b, 0:8, :] += top
            outs[k - 1][b, size - 8:size, :] += end
            start += lanes_of(cols)


def swap(value, axis):
    e, o = value
    count = lax.axis_size(axis)
    pairs = [[], []]
    for i in range(count - 1):
        pairs[i % 2] += [(i, i + 1), (i + 1, i)]
    return lax.ppermute(e, axis, pairs[0]), lax.ppermute(o, axis, pairs[1])


def solution(mesh):
    counts = (mesh.shape["row"], mesh.shape["col"])

    def local(relief):
        shape = bands, n, m = relief.shape
        levels = [jax.ShapeDtypeStruct((bands, n >> k, m >> k), F32) for k in range(1, LEVELS + 1)]
        width = sum(lanes_of(m >> k) for k in range(1, LEVELS + 1))
        row_part = jax.ShapeDtypeStruct((8, width), F32)
        col_part = jax.ShapeDtypeStruct((16, 128), F32)
        rim = jax.ShapeDtypeStruct((bands, 128, 128), F32)
        *own, rim_a, rim_b, send_e, send_o = pl.pallas_call(
            functools.partial(pyramid_kernel, shape, counts),
            out_shape=levels + [rim, rim, row_part, row_part],
            in_specs=[pl.BlockSpec(memory_space=pl.ANY)],
            out_specs=[VMEM] * 8,
            scratch_shapes=[
                pltpu.VMEM((bands, (lanes_of(m >> k) if k else m) // 128, PAD + (n >> k) + TAIL, 128), F32)
                for k in range(LEVELS)
            ] + [
                pltpu.VMEM((4, 256, 256), BF16),
                pltpu.VMEM((128, 256), BF16),
                pltpu.VMEM((m >> 2, m >> 3), BF16),
                pltpu.SemaphoreType.DMA((bands, m // 128)),
            ],
            name="pyramid",
        )(relief)
        row_e, row_o = swap((send_e, send_o), "row")
        send_e, send_o = pl.pallas_call(
            functools.partial(rim_kernel, shape),
            out_shape=[col_part, col_part],
            in_specs=[VMEM] * 4,
            out_specs=[VMEM] * 2,
            scratch_shapes=[pltpu.VMEM((bands, 128, 128), F32)] * 2,
            name="rim",
        )(rim_a, rim_b, row_e, row_o)
        col_e, col_o = swap((send_e, send_o), "col")
        return tuple(pl.pallas_call(
            functools.partial(finish_kernel, shape),
            out_shape=levels,
            in_specs=[VMEM] * 8,
            out_specs=[VMEM] * 4,
            scratch_shapes=[pltpu.VMEM((bands, 128, 128), F32)] * 2,
            name="finish",
        )(*own, row_e, row_o, col_e, col_o))

    placed = P(None, "row", "col")
    return jax.shard_map(
        local, mesh=mesh, in_specs=(placed,), out_specs=(placed,) * LEVELS, check_vma=False
    )
```

time: 352 us -> 26.2 us (0.07)
  the two profiles are of different devices: /device:TPU:3 before, /device:TPU:20 now
where the time goes in v1:
time: 26.2 us; the launch traced here: 26 us
  Pallas kernels  10.1 us (39%)
  waiting for transfers between devices  7.06 us (27%)
  starting transfers between devices  6.99 us (27%)
  local copies, waits for them, and re-layouts  1.21 us (5%)
  between operations  0.68 us (3%)
    ppermute x4, waiting for transfers between devices, swap(): return (lax.ppermute(e, axis, pairs[0]), lax.ppermute(o, axis, pairs[1]))  7.06 us
    ppermute x4, starting transfers between devices, swap(): return (lax.ppermute(e, axis, pairs[0]), lax.ppermute(o, axis, pairs[1]))  6.99 us
    pallas_call x1, Pallas kernels, local(): pl.pallas_call(functools.partial(pyramid_kernel, shape, counts), out_shap...  5.78 us
    pallas_call x1, Pallas kernels, local(): pl.pallas_call(functools.partial(finish_kernel, shape), out_shape=levels,...  2.46 us
    pallas_call x1, Pallas kernels, local(): pl.pallas_call(functools.partial(rim_kernel, shape), out_shape=[col_part,...  1.85 us
    unnamed x8, local copies, waits for them, and re-layouts  1.21 us
  transfers between devices with their start and end apart: 4, of which 3 were waited for; matrix products, arithmetic and copies ran while one was open for 0% of the time, Pallas kernels for 0%

profile of v1, /device:TPU:20, one launch (start us, length us, event | category | flops | bytes accessed | tf_op | source)
XLA Modules:
  0.0 26.0 jit_solution(17452657625085087747)
XLA Ops:
  0.6 5.8 %pyramid.1 = (f32[3,128,512]{2,1,0:T(8,128)}, f32[3,64,256]{2,1,0:T(8,128)}, f32[3,32,128]{2,1,0:T(8,128)}, f32[3,16,64]{2,1,0:T(8,128)}, f32[3,128,128]{2,1,0:T...) custom-call(f32[3,256,1024]{2,1,0:T(8,128)} %x_hbm.1), custom_call_target="tpu_custom_call" | custom-call | tf_op jit(solution)/shard_map/pyramid/pallas_call | solution.py:325
  6.4 0.1 collective-permute-start
  6.5 3.4 %collective-permute-start.1 = (f32[8,1408]{1,0:T(8,128)}, f32[8,1408]{1,0:T(8,128)S(1)}, u32[]{:S(2)}, u32[]{:S(2)}) collective-permute-start(f32[8,1408]{1,0:T(8,128)} %get-tuple-element.19), channel_id=1, source_target_pairs={{4,8},{8,4},{12,16},{16,12},{20,24},{24,20},{5,9},{9,5},{13,17},{1... | collective-permute-start | bytes 135176 | tf_op jit(solution)/shard_map/ppermute | solution.py:312
  9.9 0.0 collective-permute-done.got_e.row_e
  9.9 0.0 copy-start
  10.0 3.2 %collective-permute-done.1.got_o.row_o = f32[8,1408]{1,0:T(8,128)S(1)} collective-permute-done((f32[8,1408]{1,0:T(8,128)}, f32[8,1408]{1,0:T(8,128)S(1)}, u32[]{:S(2)}, u32[]{:S(2)}) %collective-permute-start.1) | collective-permute-done | bytes 45088 | tf_op jit(solution)/shard_map/ppermute | solution.py:312
  13.2 0.0 copy-start.1
  13.2 0.0 copy-done
  13.2 0.6 %copy-done.1 = f32[8,1408]{1,0:T(8,128)} copy-done((f32[8,1408]{1,0:T(8,128)}, f32[8,1408]{1,0:T(8,128)S(1)}, u32[]{:S(2)}) %copy-start.1) | copy-done | bytes 45080
  13.8 1.9 %rim.1 = (f32[16,128]{1,0:T(8,128)}, f32[16,128]{1,0:T(8,128)}) custom-call(f32[3,128,128]{2,1,0:T(8,128)} %get-tuple-element.20.rim_a, f32[3,128,128]{2,1,0:T(8,128)} %get-tuple-element.21.rim_b, f32[8,1408]{1,0:T(8,128)} %copy-done, f32[8,1408]{1,0:T(8,128)} %copy-done.1), custom_call_target="tpu_custom_call" | custom-call | tf_op jit(solution)/shard_map/rim/pallas_call | solution.py:342
  15.7 1.6 %collective-permute-start.2 = (f32[16,128]{1,0:T(8,128)}, f32[16,128]{1,0:T(8,128)S(1)}, u32[]{:S(2)}, u32[]{:S(2)}) collective-permute-start(f32[16,128]{1,0:T(8,128)} %get-tuple-element.22), channel_id=1, source_target_pairs={{0,1},{1,0},{2,3},{3,2},{4,5},{5,4},{6,7},{7,6},{8,9},{9,8},{10,11... | collective-permute-start | bytes 24584 | tf_op jit(solution)/shard_map/ppermute | solution.py:312
  17.2 1.9 %collective-permute-start.3 = (f32[16,128]{1,0:T(8,128)}, f32[16,128]{1,0:T(8,128)S(1)}, u32[]{:S(2)}, u32[]{:S(2)}) collective-permute-start(f32[16,128]{1,0:T(8,128)} %get-tuple-element.23), channel_id=1, source_target_pairs={{1,2},{2,1},{5,6},{6,5},{9,10},{10,9},{13,14},{14,13},{17,18},{18,... | collective-permute-start | bytes 24584 | tf_op jit(solution)/shard_map/ppermute | solution.py:312
  19.2 0.4 %collective-permute-done.2.col_e = f32[16,128]{1,0:T(8,128)S(1)} collective-permute-done((f32[16,128]{1,0:T(8,128)}, f32[16,128]{1,0:T(8,128)S(1)}, u32[]{:S(2)}, u32[]{:S(2)}) %collective-permute-start.2) | collective-permute-done | bytes 8224 | tf_op jit(solution)/shard_map/ppermute | solution.py:312
  19.5 0.0 copy-start.2
  19.5 3.5 %collective-permute-done.3.col_o = f32[16,128]{1,0:T(8,128)S(1)} collective-permute-done((f32[16,128]{1,0:T(8,128)}, f32[16,128]{1,0:T(8,128)S(1)}, u32[]{:S(2)}, u32[]{:S(2)}) %collective-permute-start.3) | collective-permute-done | bytes 8224 | tf_op jit(solution)/shard_map/ppermute | solution.py:312
  23.0 0.0 copy-start.3
  23.0 0.0 copy-done.2
  23.0 0.6 %copy-done.3 = f32[16,128]{1,0:T(8,128)} copy-done((f32[16,128]{1,0:T(8,128)}, f32[16,128]{1,0:T(8,128)S(1)}, u32[]{:S(2)}) %copy-start.3) | copy-done | bytes 8216
  23.6 2.5 %finish.1 = (f32[3,128,512]{2,1,0:T(8,128)}, f32[3,64,256]{2,1,0:T(8,128)}, f32[3,32,128]{2,1,0:T(8,128)}, f32[3,16,64]{2,1,0:T(8,128)}) custom-call(f32[3,128,512]{2,1,0:T(8,128)} %get-tuple-element.14.one, f32[3,64,256]{2,1,0:T(8,128)} %get-tuple-element.15.two, f32[3,32,128]{2,1,0:T(8,128)} %get-tuple-element.16.three, ...), custom_call_target="tpu_custom_call" | custom-call | tf_op jit(solution)/shard_map/finish/pallas_call | solution.py:351
Async XLA Ops:
  6.4 3.5 %collective-permute-start = (f32[8,1408]{1,0:T(8,128)}, f32[8,1408]{1,0:T(8,128)S(1)}, u32[]{:S(2)}, u32[]{:S(2)}) collective-permute-start(f32[8,1408]{1,0:T(8,128)} %get-tuple-element.18), channel_id=1, source_target_pairs={{0,4},{4,0},{8,12},{12,8},{16,20},{20,16},{24,28},{28,24},{1,5},{5... | collective-permute-start | bytes 135176 | tf_op jit(solution)/shard_map/ppermute | solution.py:312
  6.5 6.7 %collective-permute-start.1 = (f32[8,1408]{1,0:T(8,128)}, f32[8,1408]{1,0:T(8,128)S(1)}, u32[]{:S(2)}, u32[]{:S(2)}) collective-permute-start(f32[8,1408]{1,0:T(8,128)} %get-tuple-element.19), channel_id=1, source_target_pairs={{4,8},{8,4},{12,16},{16,12},{20,24},{24,20},{5,9},{9,5},{13,17},{1... | collective-permute-start | bytes 135176 | tf_op jit(solution)/shard_map/ppermute | solution.py:312
  9.9 3.2 %copy-start = (f32[8,1408]{1,0:T(8,128)}, f32[8,1408]{1,0:T(8,128)S(1)}, u32[]{:S(2)}) copy-start(f32[8,1408]{1,0:T(8,128)S(1)} %collective-permute-done.got_e.row_e) | copy-start | bytes 135172
  13.2 0.6 %copy-start.1 = (f32[8,1408]{1,0:T(8,128)}, f32[8,1408]{1,0:T(8,128)S(1)}, u32[]{:S(2)}) copy-start(f32[8,1408]{1,0:T(8,128)S(1)} %collective-permute-done.1.got_o.row_o) | copy-start | bytes 135172
  15.7 3.9 %collective-permute-start.2 = (f32[16,128]{1,0:T(8,128)}, f32[16,128]{1,0:T(8,128)S(1)}, u32[]{:S(2)}, u32[]{:S(2)}) collective-permute-start(f32[16,128]{1,0:T(8,128)} %get-tuple-element.22), channel_id=1, source_target_pairs={{0,1},{1,0},{2,3},{3,2},{4,5},{5,4},{6,7},{7,6},{8,9},{9,8},{10,11... | collective-permute-start | bytes 24584 | tf_op jit(solution)/shard_map/ppermute | solution.py:312
  17.2 5.7 %collective-permute-start.3 = (f32[16,128]{1,0:T(8,128)}, f32[16,128]{1,0:T(8,128)S(1)}, u32[]{:S(2)}, u32[]{:S(2)}) collective-permute-start(f32[16,128]{1,0:T(8,128)} %get-tuple-element.23), channel_id=1, source_target_pairs={{1,2},{2,1},{5,6},{6,5},{9,10},{10,9},{13,14},{14,13},{17,18},{18,... | collective-permute-start | bytes 24584 | tf_op jit(solution)/shard_map/ppermute | solution.py:312
  19.5 3.5 %copy-start.2 = (f32[16,128]{1,0:T(8,128)}, f32[16,128]{1,0:T(8,128)S(1)}, u32[]{:S(2)}) copy-start(f32[16,128]{1,0:T(8,128)S(1)} %collective-permute-done.2.col_e) | copy-start | bytes 24580
  23.0 0.6 %copy-start.3 = (f32[16,128]{1,0:T(8,128)}, f32[16,128]{1,0:T(8,128)S(1)}, u32[]{:S(2)}) copy-start(f32[16,128]{1,0:T(8,128)S(1)} %collective-permute-done.3.col_o) | copy-start | bytes 24580

commit v2 on v1

--- a/solution.py
+++ b/solution.py
@@ -11,6 +11,7 @@
 BF16 = jnp.bfloat16
 FAR = 1 << 20
 LEVELS = 4
+LIMIT = 24_000_000
 VMEM = pl.BlockSpec(memory_space=pltpu.VMEM)
 PAD = 8
 TAIL = 24
@@ -194,6 +195,7 @@
             else:
                 rim_b[b, start:start + half, :] = body
     down, up = jnp.concatenate(sum(down, []), 1), jnp.concatenate(sum(up, []), 1)
+    down, up = jnp.where(bottom, 0.0, down), jnp.where(top, 0.0, up)
     even = (row & 1) == 0
     send_e[...] = jnp.where(even, down, up)
     send_o[...] = jnp.where(even, up, down)
@@ -223,7 +225,7 @@
     return out
 
 
-def rim_kernel(shape, rim_a, rim_b, got_e, got_o, send_e, send_o, tile_a, tile_b):
+def rim_kernel(shape, counts, rim_a, rim_b, got_e, got_o, send_e, send_o, tile_a, tile_b):
     bands, n, m = shape
     above, below = from_rows(got_e, got_o)
     offsets, start = [], 0
@@ -254,7 +256,10 @@
         to_right = jnp.where(sub == 4 * b + 2, c[1:2], to_right)
         to_left = jnp.where(sub == 4 * b, a[127:128], to_left)
         to_left = jnp.where(sub == 4 * b + 1, c[127:128], to_left)
-    even = (lax.axis_index("col") & 1) == 0
+    col = lax.axis_index("col")
+    to_right = jnp.where(col == counts[1] - 1, 0.0, to_right)
+    to_left = jnp.where(col == 0, 0.0, to_left)
+    even = (col & 1) == 0
     send_e[...] = jnp.where(even, to_right, to_left)
     send_o[...] = jnp.where(even, to_left, to_right)
 
@@ -303,13 +308,25 @@
             start += lanes_of(cols)
 
 
-def swap(value, axis):
-    e, o = value
-    count = lax.axis_size(axis)
-    pairs = [[], []]
-    for i in range(count - 1):
-        pairs[i % 2] += [(i, i + 1), (i + 1, i)]
-    return lax.ppermute(e, axis, pairs[0]), lax.ppermute(o, axis, pairs[1])
+def swap(pair, axis, counts):
+    sizes = [counts[name] for name in ("row", "col")]
+    along = ("row", "col").index(axis)
+    out = []
+    for parity, value in enumerate(pair):
+        moves = []
+        for i in range(sizes[0] * sizes[1]):
+            place = list(divmod(i, sizes[1]))
+            step = 1 if place[along] % 2 == parity else -1
+            target = list(place)
+            if 0 <= place[along] + step < sizes[along]:
+                target[along] += step
+            elif (place[1 - along] ^ 1) < sizes[1 - along]:
+                target[1 - along] ^= 1
+            else:
+                continue
+            moves.append((i, target[0] * sizes[1] + target[1]))
+        out.append(lax.ppermute(value, ("row", "col"), moves))
+    return out
 
 
 def solution(mesh):
@@ -325,7 +342,7 @@
         *own, rim_a, rim_b, send_e, send_o = pl.pallas_call(
             functools.partial(pyramid_kernel, shape, counts),
             out_shape=levels + [rim, rim, row_part, row_part],
-            in_specs=[pl.BlockSpec(memory_space=pl.ANY)],
+            in_specs=[pl.BlockSpec(memory_space=pltpu.HBM)],
             out_specs=[VMEM] * 8,
             scratch_shapes=[
                 pltpu.VMEM((bands, (lanes_of(m >> k) if k else m) // 128, PAD + (n >> k) + TAIL, 128), F32)
@@ -336,24 +353,27 @@
                 pltpu.VMEM((m >> 2, m >> 3), BF16),
                 pltpu.SemaphoreType.DMA((bands, m // 128)),
             ],
+            compiler_params=pltpu.CompilerParams(vmem_limit_bytes=LIMIT),
             name="pyramid",
-        )(relief)
-        row_e, row_o = swap((send_e, send_o), "row")
+        )(pltpu.with_memory_space_constraint(relief, pltpu.HBM))
+        row_e, row_o = swap((send_e, send_o), "row", mesh.shape)
         send_e, send_o = pl.pallas_call(
-            functools.partial(rim_kernel, shape),
+            functools.partial(rim_kernel, shape, counts),
             out_shape=[col_part, col_part],
             in_specs=[VMEM] * 4,
             out_specs=[VMEM] * 2,
             scratch_shapes=[pltpu.VMEM((bands, 128, 128), F32)] * 2,
+            compiler_params=pltpu.CompilerParams(vmem_limit_bytes=4 << 20),
             name="rim",
         )(rim_a, rim_b, row_e, row_o)
-        col_e, col_o = swap((send_e, send_o), "col")
+        col_e, col_o = swap((send_e, send_o), "col", mesh.shape)
         return tuple(pl.pallas_call(
             functools.partial(finish_kernel, shape),
             out_shape=levels,
             in_specs=[VMEM] * 8,
             out_specs=[VMEM] * 4,
             scratch_shapes=[pltpu.VMEM((bands, 128, 128), F32)] * 2,
+            compiler_params=pltpu.CompilerParams(vmem_limit_bytes=8 << 20),
             name="finish",
         )(*own, row_e, row_o, col_e, col_o))
 

time: 26.2 us -> 16.9 us (0.65)
  Pallas kernels: 10.1 us -> 6.18 us
  starting transfers between devices: 6.99 us -> 3.25 us
  local copies, waits for them, and re-layouts: 1.21 us -> 0 us
  waiting for transfers between devices: 7.06 us -> 6.71 us
    ppermute x4, starting transfers between devices: 6.99 us -> 3.25 us  [swap(): out.append(lax.ppermute(value, ('row', 'col'), moves))]
    pallas_call x1, Pallas kernels: 1.85 us -> 0.2 us  [local(): pl.pallas_call(functools.partial(rim_kernel, shape, counts), out_shape=[c...]
    pallas_call x1, Pallas kernels: 2.46 us -> 1.16 us  [local(): pl.pallas_call(functools.partial(finish_kernel, shape), out_shape=levels,...]
    unnamed x8 -> x0, local copies, waits for them, and re-layouts: 1.21 us -> none
    pallas_call x1, Pallas kernels: 5.78 us -> 4.82 us  [local(): pl.pallas_call(functools.partial(pyramid_kernel, shape, counts), out_shap...]
    ppermute x4, waiting for transfers between devices: 7.06 us -> 6.71 us  [swap(): out.append(lax.ppermute(value, ('row', 'col'), moves))]
where the time goes in v2:
time: 16.9 us; the launch traced here: 16.8 us
  waiting for transfers between devices  6.71 us (40%)
  Pallas kernels  6.18 us (37%)
  starting transfers between devices  3.25 us (19%)
  between operations  0.66 us (4%)
    ppermute x4, waiting for transfers between devices, swap(): out.append(lax.ppermute(value, ('row', 'col'), moves))  6.71 us
    pallas_call x1, Pallas kernels, local(): pl.pallas_call(functools.partial(pyramid_kernel, shape, counts), out_shap...  4.82 us
    ppermute x4, starting transfers between devices, swap(): out.append(lax.ppermute(value, ('row', 'col'), moves))  3.25 us
    pallas_call x1, Pallas kernels, local(): pl.pallas_call(functools.partial(finish_kernel, shape), out_shape=levels,...  1.16 us
  transfers between devices with their start and end apart: 4, of which 3 were waited for; matrix products, arithmetic and copies ran while one was open for 0% of the time, Pallas kernels for 0%

profile of v2, /device:TPU:20, one launch (start us, length us, event | category | flops | bytes accessed | tf_op | source)
XLA Modules:
  0.0 16.8 jit_solution(7510184542992829704)
XLA Ops:
  0.6 4.8 %pyramid.1 = (f32[3,128,512]{2,1,0:T(8,128)S(1)}, f32[3,64,256]{2,1,0:T(8,128)S(1)}, f32[3,32,128]{2,1,0:T(8,128)S(1)}, f32[3,16,64]{2,1,0:T(8,128)S(1)}, f32[3,...) custom-call(f32[3,256,1024]{2,1,0:T(8,128)} %x_hbm.1), custom_call_target="tpu_custom_call" | custom-call | tf_op jit(solution)/shard_map/pyramid/pallas_call | solution.py:342
  5.5 0.1 collective-permute-start
  5.5 1.5 %collective-permute-start.1 = (f32[8,1408]{1,0:T(8,128)S(1)}, f32[8,1408]{1,0:T(8,128)S(1)}, u32[]{:S(2)}, u32[]{:S(2)}) collective-permute-start(f32[8,1408]{1,0:T(8,128)S(1)} %get-tuple-element.19), channel_id=1, source_target_pairs={{0,1},{1,0},{2,3},{3,2},{4,8},{5,9},{6,10},{7,11},{8,4},{9,5},{10,... | collective-permute-start | bytes 135176 | tf_op jit(solution)/shard_map/ppermute | solution.py:328
  7.1 0.0 collective-permute-done.got_e.row_e
  7.1 3.1 %collective-permute-done.1.got_o.row_o = f32[8,1408]{1,0:T(8,128)S(1)} collective-permute-done((f32[8,1408]{1,0:T(8,128)S(1)}, f32[8,1408]{1,0:T(8,128)S(1)}, u32[]{:S(2)}, u32[]{:S(2)}) %collective-permute-start.1) | collective-permute-done | bytes 45088 | tf_op jit(solution)/shard_map/ppermute | solution.py:328
  10.1 0.2 %rim.1 = (f32[16,128]{1,0:T(8,128)S(1)}, f32[16,128]{1,0:T(8,128)S(1)}) custom-call(f32[3,128,128]{2,1,0:T(8,128)S(1)} %get-tuple-element.20.rim_a, f32[3,128,128]{2,1,0:T(8,128)S(1)} %get-tuple-element.21.rim_b, f32[8,1408]{1,0:T(8,128)S(1)} %collective-permute-done.got_e.row_e, f32[8,1408]{1,0:T(8,128)S(1)} %collective-permute-done.1.got_o.row_o), custom_call_target="tpu_custom_call" | custom-call | tf_op jit(solution)/shard_map/rim/pallas_call | solution.py:360
  10.3 1.6 %collective-permute-start.2 = (f32[16,128]{1,0:T(8,128)S(1)}, f32[16,128]{1,0:T(8,128)S(1)}, u32[]{:S(2)}, u32[]{:S(2)}) collective-permute-start(f32[16,128]{1,0:T(8,128)S(1)} %get-tuple-element.22), channel_id=1, source_target_pairs={{0,1},{1,0},{2,3},{3,2},{4,5},{5,4},{6,7},{7,6},{8,9},{9,8},{10,11... | collective-permute-start | bytes 24584 | tf_op jit(solution)/shard_map/ppermute | solution.py:328
  12.0 0.0 collective-permute-start.3
  12.0 2.1 %collective-permute-done.2.col_e = f32[16,128]{1,0:T(8,128)S(1)} collective-permute-done((f32[16,128]{1,0:T(8,128)S(1)}, f32[16,128]{1,0:T(8,128)S(1)}, u32[]{:S(2)}, u32[]{:S(2)}) %collective-permute-start.2) | collective-permute-done | bytes 8224 | tf_op jit(solution)/shard_map/ppermute | solution.py:328
  14.1 1.6 %collective-permute-done.3.col_o = f32[16,128]{1,0:T(8,128)S(1)} collective-permute-done((f32[16,128]{1,0:T(8,128)S(1)}, f32[16,128]{1,0:T(8,128)S(1)}, u32[]{:S(2)}, u32[]{:S(2)}) %collective-permute-start.3) | collective-permute-done | bytes 8224 | tf_op jit(solution)/shard_map/ppermute | solution.py:328
  15.6 1.2 %finish.1 = (f32[3,128,512]{2,1,0:T(8,128)}, f32[3,64,256]{2,1,0:T(8,128)}, f32[3,32,128]{2,1,0:T(8,128)}, f32[3,16,64]{2,1,0:T(8,128)}) custom-call(f32[3,128,512]{2,1,0:T(8,128)S(1)} %get-tuple-element.14.one, f32[3,64,256]{2,1,0:T(8,128)S(1)} %get-tuple-element.15.two, f32[3,32,128]{2,1,0:T(8,128)S(1)} %get-tuple-element.16.three, ...), custom_call_target="tpu_custom_call" | custom-call | tf_op jit(solution)/shard_map/finish/pallas_call | solution.py:370
Async XLA Ops:
  5.5 1.6 %collective-permute-start = (f32[8,1408]{1,0:T(8,128)S(1)}, f32[8,1408]{1,0:T(8,128)S(1)}, u32[]{:S(2)}, u32[]{:S(2)}) collective-permute-start(f32[8,1408]{1,0:T(8,128)S(1)} %get-tuple-element.18), channel_id=1, source_target_pairs={{0,4},{1,5},{2,6},{3,7},{4,0},{5,1},{6,2},{7,3},{8,12},{9,13},{10,... | collective-permute-start | bytes 135176 | tf_op jit(solution)/shard_map/ppermute | solution.py:328
  5.5 4.6 %collective-permute-start.1 = (f32[8,1408]{1,0:T(8,128)S(1)}, f32[8,1408]{1,0:T(8,128)S(1)}, u32[]{:S(2)}, u32[]{:S(2)}) collective-permute-start(f32[8,1408]{1,0:T(8,128)S(1)} %get-tuple-element.19), channel_id=1, source_target_pairs={{0,1},{1,0},{2,3},{3,2},{4,8},{5,9},{6,10},{7,11},{8,4},{9,5},{10,... | collective-permute-start | bytes 135176 | tf_op jit(solution)/shard_map/ppermute | solution.py:328
  10.3 3.7 %collective-permute-start.2 = (f32[16,128]{1,0:T(8,128)S(1)}, f32[16,128]{1,0:T(8,128)S(1)}, u32[]{:S(2)}, u32[]{:S(2)}) collective-permute-start(f32[16,128]{1,0:T(8,128)S(1)} %get-tuple-element.22), channel_id=1, source_target_pairs={{0,1},{1,0},{2,3},{3,2},{4,5},{5,4},{6,7},{7,6},{8,9},{9,8},{10,11... | collective-permute-start | bytes 24584 | tf_op jit(solution)/shard_map/ppermute | solution.py:328
  12.0 3.7 %collective-permute-start.3 = (f32[16,128]{1,0:T(8,128)S(1)}, f32[16,128]{1,0:T(8,128)S(1)}, u32[]{:S(2)}, u32[]{:S(2)}) collective-permute-start(f32[16,128]{1,0:T(8,128)S(1)} %get-tuple-element.23), channel_id=1, source_target_pairs={{0,4},{1,2},{2,1},{3,7},{4,0},{5,6},{6,5},{7,3},{8,12},{9,10},{10,... | collective-permute-start | bytes 24584 | tf_op jit(solution)/shard_map/ppermute | solution.py:328

commit v3 on v2

--- a/solution.py
+++ b/solution.py
@@ -30,15 +30,23 @@
     return jnp.where(far == 0, 0.375, jnp.where(far == 1, 0.25, jnp.where(far == 2, 0.0625, 0.0))).astype(F32)
 
 
-def block_matrix(first, last):
+def fill_blocks(mats, first, last):
     source, lane = iota((256, 256), 0), iota((256, 256), 1)
     target = jnp.where(lane <= 128, lane, jnp.where(lane == 255, -1, FAR))
     value = band(source, target)
-    if first is not None:
-        value += first * jnp.where(source >= 1, band(-source, target), 0.0)
-    if last is not None:
-        value += last * jnp.where(source == 254, band(source + 2, target), 0.0)
-    return value.astype(BF16)
+    inside = value.astype(BF16)
+    for i in range(4):
+        mats[i] = inside
+    source, target = iota((16, 128), 0), iota((16, 128), 1)
+    mirror = jnp.where(source >= 1, band(-source, target), 0.0)
+    start = (value[:16, :128] + first * mirror).astype(BF16)
+    source = source + 240
+    mirror = jnp.where(source == 254, band(source + 2, target), 0.0)
+    end = (value[240:, :128] + last * mirror).astype(BF16)
+    for i in (1, 3):
+        mats[i, :16, :128] = start
+    for i in (2, 3):
+        mats[i, 240:, :128] = end
 
 
 def rim_matrix(first, last):
@@ -122,52 +130,114 @@
         ref[:, PAD + extent:PAD + extent + 1, :] = ref[:, PAD + extent - 2:PAD + extent - 1, :]
 
 
-def pyramid_kernel(
-    shape, counts, x_hbm, one, two, three, four, rim_a, rim_b, send_e, send_o,
-    s0, s1, s2, s3, mats, rim_mat, end_mat, sems,
+HEAD, FOOT = 16, 32
+
+
+def edge_kernel(
+    shape, counts, x_hbm, send_e, send_o, s0, mats, rim_mat, end_mat,
+    raw, e0, e1, e2, e3, down, up, edge_sems, sems,
 ):
     bands, n, m = shape
     row, col = lax.axis_index("row"), lax.axis_index("col")
     top, bottom = row == 0, row == counts[0] - 1
-    copies = [
-        [
-            pltpu.make_async_copy(
-                x_hbm.at[b, :, pl.ds(128 * t, 128)], s0.at[b, t, pl.ds(PAD, n), :], sems.at[b, t]
-            )
-            for t in range(m // 128)
-        ]
-        for b in range(bands)
+    near = [
+        pltpu.make_async_copy(x_hbm.at[:, pl.ds(0, HEAD), :], raw.at[:, pl.ds(0, HEAD), :], edge_sems.at[0]),
+        pltpu.make_async_copy(x_hbm.at[:, pl.ds(n - FOOT, FOOT), :], raw.at[:, pl.ds(HEAD, FOOT), :], edge_sems.at[1]),
     ]
-    for copy in sum(copies, []):
+    whole = [
+        pltpu.make_async_copy(
+            x_hbm.at[:, :, pl.ds(128 * t, 128)], s0.at[:, t, pl.ds(PAD, n), :], sems.at[t]
+        )
+        for t in range(m // 128)
+    ]
+    for copy in near + whole:
         copy.start()
     left = jnp.where(col == 0, 1.0, 0.0).astype(F32)
     right = jnp.where(col == counts[1] - 1, 1.0, 0.0).astype(F32)
-    mats[0] = block_matrix(None, None)
-    mats[1] = block_matrix(left, None)
-    mats[2] = block_matrix(None, right)
-    mats[3] = block_matrix(left, right)
+    fill_blocks(mats, left, right)
     rim_mat[...] = rim_matrix(left, right)
     end_mat[...] = last_matrix(end_mat.shape[1], left, right)
     matrices = [mats.at[i] for i in range(4)] + [rim_mat]
+    s0[:, :, 0:PAD, :] = jnp.zeros(s0.shape[:2] + (PAD, 128), F32)
+    s0[:, :, PAD + n:, :] = jnp.zeros(s0.shape[:2] + (TAIL, 128), F32)
+    down[...] = jnp.zeros_like(down)
+    up[...] = jnp.zeros_like(up)
+    strides = [64, 40, 40, 40]
+    for ref, stride, filled in zip((e0, e1, e2, e3), strides, (48, 24, 16, 16)):
+        for b in range(bands):
+            ref[:, stride * b:stride * b + 8, :] = jnp.zeros((ref.shape[0], 8, 128), F32)
+            rest = stride - 8 - filled
+            ref[:, stride * (b + 1) - rest:stride * (b + 1), :] = jnp.zeros((ref.shape[0], rest, 128), F32)
+    for copy in near:
+        copy.wait()
+    for b in range(bands):
+        for t in range(m // 128):
+            e0[t, 64 * b + 8:64 * b + 56, :] = raw[b, :, 128 * t:128 * t + 128]
+    lane0 = 0
+    for k, ref in enumerate((e0, e1, e2, e3)):
+        stride = strides[k]
+        head, foot, size = ((4, 24, 16), (5, 17, 8), (5, 16, 8), (5, 16, 8))[k]
+
+        def reduced(t, start, size):
+            e = [ref[t, pl.ds(start + i, size, stride=2), :] for i in range(5)]
+            return 0.0625 * (e[0] + e[4]) + 0.25 * (e[1] + e[3]) + 0.375 * e[2]
+
+        tiles = [
+            jnp.concatenate(
+                [
+                    part for b in range(bands) for part in (
+                        reduced(t, stride * b + head, 8), reduced(t, stride * b + foot, size)
+                    )
+                ],
+                0,
+            )
+            for t in range(ref.shape[0])
+        ]
+        if k < LEVELS - 1:
+            tiles = columns(tiles, m >> k, matrices)
+        else:
+            tiles = [split_dot(jnp.concatenate(tiles, 1), end_mat[...])]
+        held = 8 + size
+        first, count = ((23, 1), (14, 2), (10, 2), (8, 2))[k]
+        for t, tile in enumerate(tiles):
+            wide = pl.ds(lane0, 128)
+            for b in range(bands):
+                if k < LEVELS - 1:
+                    stride_after = strides[k + 1]
+                    (e1, e2, e3)[k][t, stride_after * b + 8:stride_after * b + 8 + held, :] = tile[held * b:held * b + held]
+                down[2 * b:2 * b + count, wide] = tile[held * b + first:held * b + first + count]
+                up[2 * b:2 * b + 1, wide] = tile[held * b:held * b + 1]
+            lane0 += 128
+    lower_part = jnp.where(bottom, 0.0, down[...])
+    upper_part = jnp.where(top, 0.0, up[...])
+    even = (row & 1) == 0
+    send_e[...] = jnp.where(even, lower_part, upper_part)
+    send_o[...] = jnp.where(even, upper_part, lower_part)
+    for copy in whole:
+        copy.wait()
+    for b in range(bands):
+        close(s0.at[b], n, top, bottom)
+
+
+def pyramid_kernel(
+    shape, counts, s0, mats, rim_mat, end_mat, one, two, three, four, rim_a, rim_b, s1, s2, s3,
+):
+    bands, n, m = shape
+    row = lax.axis_index("row")
+    top, bottom = row == 0, row == counts[0] - 1
+    matrices = [mats.at[i] for i in range(4)] + [rim_mat]
     fields, outs = [s0, s1, s2, s3], [one, two, three, four]
-    for k, ref in enumerate(fields):
-        extent = n >> k
-        skip = 0 if k == 0 else 8
-        if k == 0:
-            ref[:, :, 0:PAD, :] = jnp.zeros(ref.shape[:2] + (PAD, 128), F32)
-        ref[:, :, PAD + extent + skip:, :] = jnp.zeros(ref.shape[:2] + (TAIL - skip, 128), F32)
+    for k in range(1, LEVELS):
+        ref, extent = fields[k], n >> k
+        ref[:, :, PAD + extent + 8:, :] = jnp.zeros(ref.shape[:2] + (TAIL - 8, 128), F32)
     rim_b[...] = jnp.zeros_like(rim_b)
-    down = [[jnp.zeros((8, 128), F32)] * (lanes_of(m >> (k + 1)) // 128) for k in range(LEVELS)]
-    up = [list(d) for d in down]
     sub = iota((8, 128), 0)
     for k in range(LEVELS):
         extent, cols = n >> k, m >> k
         half = extent // 2
         for b in range(bands):
-            if k == 0:
-                for copy in copies[b]:
-                    copy.wait()
-            close(fields[k].at[b], extent, top, bottom)
+            if k:
+                close(fields[k].at[b], extent, top, bottom)
             tiles = [rows(fields[k].at[b, t], extent) for t in range(fields[k].shape[1])]
             if k < LEVELS - 1:
                 tiles = columns(tiles, cols, matrices)
@@ -182,9 +252,6 @@
                     after[b, t, PAD + half:PAD + half + 8, :] = jnp.where(sub < 2, tail, 0.0)
                     if t < len(tiles) - 1:
                         outs[k][b, :, 128 * t:128 * t + 128] = body
-                moved = pltpu.roll(tail, 2 * b, 0) if b else tail
-                down[k][t] = jnp.where((sub >= 2 * b) & (sub < 2 * b + 2), moved, down[k][t])
-                up[k][t] = jnp.where(sub == 2 * b, pltpu.roll(tail, 2 * b + 1, 0), up[k][t])
             body = tiles[-1][:half]
             start = sum(n >> j for j in range(2, k + 1))
             if k == LEVELS - 1:
@@ -194,11 +261,6 @@
                 rim_a[b] = body
             else:
                 rim_b[b, start:start + half, :] = body
-    down, up = jnp.concatenate(sum(down, []), 1), jnp.concatenate(sum(up, []), 1)
-    down, up = jnp.where(bottom, 0.0, down), jnp.where(top, 0.0, up)
-    even = (row & 1) == 0
-    send_e[...] = jnp.where(even, down, up)
-    send_o[...] = jnp.where(even, up, down)
 
 
 def from_rows(got_e, got_o):
@@ -339,23 +401,44 @@
         row_part = jax.ShapeDtypeStruct((8, width), F32)
         col_part = jax.ShapeDtypeStruct((16, 128), F32)
         rim = jax.ShapeDtypeStruct((bands, 128, 128), F32)
-        *own, rim_a, rim_b, send_e, send_o = pl.pallas_call(
-            functools.partial(pyramid_kernel, shape, counts),
-            out_shape=levels + [rim, rim, row_part, row_part],
+        tall = [
+            jax.ShapeDtypeStruct((bands, (lanes_of(m >> k) if k else m) // 128, PAD + (n >> k) + TAIL, 128), F32)
+            for k in range(LEVELS)
+        ]
+        send_e, send_o, field, *mats = pl.pallas_call(
+            functools.partial(edge_kernel, shape, counts),
+            out_shape=[
+                row_part, row_part, tall[0],
+                jax.ShapeDtypeStruct((4, 256, 256), BF16),
+                jax.ShapeDtypeStruct((128, 256), BF16),
+                jax.ShapeDtypeStruct((m >> 2, m >> 3), BF16),
+            ],
             in_specs=[pl.BlockSpec(memory_space=pltpu.HBM)],
-            out_specs=[VMEM] * 8,
+            out_specs=[VMEM] * 6,
             scratch_shapes=[
-                pltpu.VMEM((bands, (lanes_of(m >> k) if k else m) // 128, PAD + (n >> k) + TAIL, 128), F32)
-                for k in range(LEVELS)
+                pltpu.VMEM((bands, HEAD + FOOT, m), F32),
+                pltpu.VMEM((m // 128, bands * 64, 128), F32),
             ] + [
-                pltpu.VMEM((4, 256, 256), BF16),
-                pltpu.VMEM((128, 256), BF16),
-                pltpu.VMEM((m >> 2, m >> 3), BF16),
-                pltpu.SemaphoreType.DMA((bands, m // 128)),
+                pltpu.VMEM((lanes_of(m >> k) // 128, bands * 40, 128), F32) for k in range(1, LEVELS)
+            ] + [
+                pltpu.VMEM((8, width), F32),
+                pltpu.VMEM((8, width), F32),
+                pltpu.SemaphoreType.DMA((2,)),
+                pltpu.SemaphoreType.DMA((m // 128,)),
             ],
             compiler_params=pltpu.CompilerParams(vmem_limit_bytes=LIMIT),
+            name="edge",
+        )(pltpu.with_memory_space_constraint(relief, pltpu.HBM))
+        *own, rim_a, rim_b = pl.pallas_call(
+            functools.partial(pyramid_kernel, shape, counts),
+            out_shape=levels + [rim, rim],
+            in_specs=[VMEM] * 4,
+            out_specs=[VMEM] * 6,
+            scratch_shapes=[pltpu.VMEM(t.shape, F32) for t in tall[1:]],
+            compiler_params=pltpu.CompilerParams(vmem_limit_bytes=LIMIT),
+            cost_estimate=pl.CostEstimate(flops=8_000_000_000, bytes_accessed=0, transcendentals=0),
             name="pyramid",
-        )(pltpu.with_memory_space_constraint(relief, pltpu.HBM))
+        )(field, *mats)
         row_e, row_o = swap((send_e, send_o), "row", mesh.shape)
         send_e, send_o = pl.pallas_call(
             functools.partial(rim_kernel, shape, counts),

time: 16.9 us -> 14.4 us (0.85)
  waiting for transfers between devices: 6.71 us -> 3.68 us
  Pallas kernels: 6.18 us -> 6.6 us
    ppermute x4, waiting for transfers between devices: 6.71 us -> 3.68 us  [swap(): out.append(lax.ppermute(value, ('row', 'col'), moves))]
    pallas_call x0 -> x1, Pallas kernels: none -> 2.2 us  [local(): pl.pallas_call(functools.partial(edge_kernel, shape, counts), out_shape=[...]
    pallas_call x1, Pallas kernels: 4.82 us -> 3.03 us  [local(): pl.pallas_call(functools.partial(pyramid_kernel, shape, counts), out_shap...]
  transfers between devices with their start and end apart: 4 -> 4, of which waited for: 3 -> 2; matrix products, arithmetic and copies ran while one was open for 0% -> 0% of each run, Pallas kernels for 0% -> 21%
where the time goes in v3:
time: 14.4 us; the launch traced here: 14.2 us
  Pallas kernels  6.6 us (46%)
  waiting for transfers between devices  3.68 us (26%)
  starting transfers between devices  3.25 us (23%)
  between operations  0.66 us (5%)
    ppermute x4, waiting for transfers between devices, swap(): out.append(lax.ppermute(value, ('row', 'col'), moves))  3.68 us
    ppermute x4, starting transfers between devices, swap(): out.append(lax.ppermute(value, ('row', 'col'), moves))  3.25 us
    pallas_call x1, Pallas kernels, local(): pl.pallas_call(functools.partial(pyramid_kernel, shape, counts), out_shap...  3.03 us
    pallas_call x1, Pallas kernels, local(): pl.pallas_call(functools.partial(edge_kernel, shape, counts), out_shape=[...  2.2 us
    pallas_call x1, Pallas kernels, local(): pl.pallas_call(functools.partial(finish_kernel, shape), out_shape=levels,...  1.16 us
  transfers between devices with their start and end apart: 4, of which 2 were waited for; matrix products, arithmetic and copies ran while one was open for 0% of the time, Pallas kernels for 21%

profile of v3, /device:TPU:20, one launch (start us, length us, event | category | flops | bytes accessed | tf_op | source)
XLA Modules:
  0.0 14.2 jit_solution(7803140060936487377)
XLA Ops:
  0.6 2.2 %edge.1 = (f32[8,1408]{1,0:T(8,128)S(1)}, f32[8,1408]{1,0:T(8,128)S(1)}, f32[3,8,288,128]{3,2,1,0:T(8,128)S(1)}, bf16[4,256,256]{2,1,0:T(8,128)(2,1)S(1)}, bf16[...) custom-call(f32[3,256,1024]{2,1,0:T(8,128)} %x_hbm.1), custom_call_target="tpu_custom_call" | custom-call | tf_op jit(solution)/shard_map/edge/pallas_call | solution.py:408
  2.8 0.1 collective-permute-start
  2.9 1.5 %collective-permute-start.1 = (f32[8,1408]{1,0:T(8,128)S(1)}, f32[8,1408]{1,0:T(8,128)S(1)}, u32[]{:S(2)}, u32[]{:S(2)}) collective-permute-start(f32[8,1408]{1,0:T(8,128)S(1)} %get-tuple-element.27), channel_id=1, source_target_pairs={{0,1},{1,0},{2,3},{3,2},{4,8},{5,9},{6,10},{7,11},{8,4},{9,5},{10,... | collective-permute-start | bytes 135176 | tf_op jit(solution)/shard_map/ppermute | solution.py:390
  4.5 3.0 %pyramid.1 = (f32[3,128,512]{2,1,0:T(8,128)S(1)}, f32[3,64,256]{2,1,0:T(8,128)S(1)}, f32[3,32,128]{2,1,0:T(8,128)S(1)}, f32[3,16,64]{2,1,0:T(8,128)S(1)}, f32[3,...) custom-call(f32[3,8,288,128]{3,2,1,0:T(8,128)S(1)} %get-tuple-element.18.s0, ...), custom_call_target="tpu_custom_call" | custom-call | flops 8000000000 | tf_op jit(solution)/shard_map/pyramid/pallas_call | solution.py:432
  7.5 0.0 collective-permute-done.got_e.row_e
  7.5 0.0 collective-permute-done.1.got_o.row_o
  7.5 0.2 %rim.1 = (f32[16,128]{1,0:T(8,128)S(1)}, f32[16,128]{1,0:T(8,128)S(1)}) custom-call(f32[3,128,128]{2,1,0:T(8,128)S(1)} %get-tuple-element.28.rim_a, f32[3,128,128]{2,1,0:T(8,128)S(1)} %get-tuple-element.29.rim_b, f32[8,1408]{1,0:T(8,128)S(1)} %collective-permute-done.got_e.row_e, f32[8,1408]{1,0:T(8,128)S(1)} %collective-permute-done.1.got_o.row_o), custom_call_target="tpu_custom_call" | custom-call | tf_op jit(solution)/shard_map/rim/pallas_call | solution.py:443
  7.7 1.6 %collective-permute-start.2 = (f32[16,128]{1,0:T(8,128)S(1)}, f32[16,128]{1,0:T(8,128)S(1)}, u32[]{:S(2)}, u32[]{:S(2)}) collective-permute-start(f32[16,128]{1,0:T(8,128)S(1)} %get-tuple-element.30), channel_id=1, source_target_pairs={{0,1},{1,0},{2,3},{3,2},{4,5},{5,4},{6,7},{7,6},{8,9},{9,8},{10,11... | collective-permute-start | bytes 24584 | tf_op jit(solution)/shard_map/ppermute | solution.py:390
  9.4 0.0 collective-permute-start.3
  9.4 2.1 %collective-permute-done.2.col_e = f32[16,128]{1,0:T(8,128)S(1)} collective-permute-done((f32[16,128]{1,0:T(8,128)S(1)}, f32[16,128]{1,0:T(8,128)S(1)}, u32[]{:S(2)}, u32[]{:S(2)}) %collective-permute-start.2) | collective-permute-done | bytes 8224 | tf_op jit(solution)/shard_map/ppermute | solution.py:390
  11.4 1.6 %collective-permute-done.3.col_o = f32[16,128]{1,0:T(8,128)S(1)} collective-permute-done((f32[16,128]{1,0:T(8,128)S(1)}, f32[16,128]{1,0:T(8,128)S(1)}, u32[]{:S(2)}, u32[]{:S(2)}) %collective-permute-start.3) | collective-permute-done | bytes 8224 | tf_op jit(solution)/shard_map/ppermute | solution.py:390
  13.0 1.2 %finish.1 = (f32[3,128,512]{2,1,0:T(8,128)}, f32[3,64,256]{2,1,0:T(8,128)}, f32[3,32,128]{2,1,0:T(8,128)}, f32[3,16,64]{2,1,0:T(8,128)}) custom-call(f32[3,128,512]{2,1,0:T(8,128)S(1)} %get-tuple-element.22.one, f32[3,64,256]{2,1,0:T(8,128)S(1)} %get-tuple-element.23.two, f32[3,32,128]{2,1,0:T(8,128)S(1)} %get-tuple-element.24.three, ...), custom_call_target="tpu_custom_call" | custom-call | tf_op jit(solution)/shard_map/finish/pallas_call | solution.py:453
Async XLA Ops:
  2.8 4.6 %collective-permute-start = (f32[8,1408]{1,0:T(8,128)S(1)}, f32[8,1408]{1,0:T(8,128)S(1)}, u32[]{:S(2)}, u32[]{:S(2)}) collective-permute-start(f32[8,1408]{1,0:T(8,128)S(1)} %get-tuple-element.26), channel_id=1, source_target_pairs={{0,4},{1,5},{2,6},{3,7},{4,0},{5,1},{6,2},{7,3},{8,12},{9,13},{10,... | collective-permute-start | bytes 135176 | tf_op jit(solution)/shard_map/ppermute | solution.py:390
  2.9 4.6 %collective-permute-start.1 = (f32[8,1408]{1,0:T(8,128)S(1)}, f32[8,1408]{1,0:T(8,128)S(1)}, u32[]{:S(2)}, u32[]{:S(2)}) collective-permute-start(f32[8,1408]{1,0:T(8,128)S(1)} %get-tuple-element.27), channel_id=1, source_target_pairs={{0,1},{1,0},{2,3},{3,2},{4,8},{5,9},{6,10},{7,11},{8,4},{9,5},{10,... | collective-permute-start | bytes 135176 | tf_op jit(solution)/shard_map/ppermute | solution.py:390
  7.7 3.7 %collective-permute-start.2 = (f32[16,128]{1,0:T(8,128)S(1)}, f32[16,128]{1,0:T(8,128)S(1)}, u32[]{:S(2)}, u32[]{:S(2)}) collective-permute-start(f32[16,128]{1,0:T(8,128)S(1)} %get-tuple-element.30), channel_id=1, source_target_pairs={{0,1},{1,0},{2,3},{3,2},{4,5},{5,4},{6,7},{7,6},{8,9},{9,8},{10,11... | collective-permute-start | bytes 24584 | tf_op jit(solution)/shard_map/ppermute | solution.py:390
  9.4 3.7 %collective-permute-start.3 = (f32[16,128]{1,0:T(8,128)S(1)}, f32[16,128]{1,0:T(8,128)S(1)}, u32[]{:S(2)}, u32[]{:S(2)}) collective-permute-start(f32[16,128]{1,0:T(8,128)S(1)} %get-tuple-element.31), channel_id=1, source_target_pairs={{0,4},{1,2},{2,1},{3,7},{4,0},{5,6},{6,5},{7,3},{8,12},{9,10},{10,... | collective-permute-start | bytes 24584 | tf_op jit(solution)/shard_map/ppermute | solution.py:390

commit v4 on v3

--- a/solution.py
+++ b/solution.py
@@ -6,6 +6,7 @@
 from jax.experimental import pallas as pl
 from jax.experimental.pallas import tpu as pltpu
 from jax.sharding import PartitionSpec as P
+
 
 F32 = jnp.float32
 BF16 = jnp.bfloat16
@@ -227,40 +228,53 @@
     top, bottom = row == 0, row == counts[0] - 1
     matrices = [mats.at[i] for i in range(4)] + [rim_mat]
     fields, outs = [s0, s1, s2, s3], [one, two, three, four]
+    sub = iota((8, 128), 0)
+
+    def store(k, b, t, tile):
+        half = n >> (k + 1)
+        tail, after = tile[half:], fields[k + 1]
+        after[b, t, PAD:PAD + half, :] = tile[:half]
+        after[b, t, 0:PAD, :] = jnp.where(sub == 7, tail, 0.0)
+        after[b, t, PAD + half:PAD + half + 8, :] = jnp.where(sub < 2, tail, 0.0)
+        after[b, t, PAD + half + 8:, :] = jnp.zeros((TAIL - 8, 128), F32)
+        if 128 * t < outs[k].shape[2]:
+            outs[k][b, :, 128 * t:128 * t + 128] = tile[:half]
+        elif k == 0:
+            rim_a[b] = tile[:half]
+
+    def level_one(b, _):
+        tiles = columns([rows(s0.at[b, t], n) for t in range(m // 128)], m, matrices)
+        for t, tile in enumerate(tiles):
+            store(0, b, t, tile)
+        return 0
+
+    lax.fori_loop(0, bands, level_one, 0)
+    start = 0
     for k in range(1, LEVELS):
-        ref, extent = fields[k], n >> k
-        ref[:, :, PAD + extent + 8:, :] = jnp.zeros(ref.shape[:2] + (TAIL - 8, 128), F32)
-    rim_b[...] = jnp.zeros_like(rim_b)
-    sub = iota((8, 128), 0)
-    for k in range(LEVELS):
         extent, cols = n >> k, m >> k
         half = extent // 2
         for b in range(bands):
-            if k:
-                close(fields[k].at[b], extent, top, bottom)
-            tiles = [rows(fields[k].at[b, t], extent) for t in range(fields[k].shape[1])]
+            close(fields[k].at[b], extent, top, bottom)
+        tiles = [
+            jnp.concatenate([rows(fields[k].at[b, t], extent) for b in range(bands)], 0)
+            for t in range(fields[k].shape[1])
+        ]
+        if k < LEVELS - 1:
+            tiles = columns(tiles, cols, matrices)
+        else:
+            tiles = [split_dot(jnp.concatenate(tiles, 1), end_mat[...])]
+        for b in range(bands):
+            parts = [tile[(half + 8) * b:(half + 8) * (b + 1)] for tile in tiles]
+            body = parts[-1][:half]
             if k < LEVELS - 1:
-                tiles = columns(tiles, cols, matrices)
+                for t, tile in enumerate(parts):
+                    store(k, b, t, tile)
             else:
-                tiles = [split_dot(jnp.concatenate(tiles, 1), end_mat[...])]
-            for t, tile in enumerate(tiles):
-                body, tail = tile[:half], tile[half:]
-                if k < LEVELS - 1:
-                    after = fields[k + 1]
-                    after[b, t, PAD:PAD + half, :] = body
-                    after[b, t, 0:PAD, :] = jnp.where(sub == 7, tail, 0.0)
-                    after[b, t, PAD + half:PAD + half + 8, :] = jnp.where(sub < 2, tail, 0.0)
-                    if t < len(tiles) - 1:
-                        outs[k][b, :, 128 * t:128 * t + 128] = body
-            body = tiles[-1][:half]
-            start = sum(n >> j for j in range(2, k + 1))
-            if k == LEVELS - 1:
                 four[b] = body[:, :cols // 2]
                 body = jnp.where(iota(body.shape, 1) < 2, pltpu.roll(body, 128 - cols // 2, 1), body)
-            if k == 0:
-                rim_a[b] = body
-            else:
-                rim_b[b, start:start + half, :] = body
+            rim_b[b, start:start + half, :] = body
+        start += half
+    rim_b[:, start:, :] = jnp.zeros((bands, 128 - start, 128), F32)
 
 
 def from_rows(got_e, got_o):
@@ -287,7 +301,9 @@
     return out
 
 
-def rim_kernel(shape, counts, rim_a, rim_b, got_e, got_o, send_e, send_o, tile_a, tile_b):
+def rim_kernel(
+    shape, counts, rim_a, rim_b, got_e, got_o, send_0, send_1, send_2, tile_a, tile_b
+):
     bands, n, m = shape
     above, below = from_rows(got_e, got_o)
     offsets, start = [], 0
@@ -321,20 +337,21 @@
     col = lax.axis_index("col")
     to_right = jnp.where(col == counts[1] - 1, 0.0, to_right)
     to_left = jnp.where(col == 0, 0.0, to_left)
-    even = (col & 1) == 0
-    send_e[...] = jnp.where(even, to_right, to_left)
-    send_o[...] = jnp.where(even, to_left, to_right)
+    for k, send in enumerate((send_0, send_1, send_2)):
+        left = jnp.where((col + 2) % 3 == k, to_left, 0.0)
+        send[...] = jnp.where(col % 3 == k, to_right, left)
 
 
 def finish_kernel(
-    shape, one, two, three, four, row_e, row_o, col_e, col_o,
+    shape, one, two, three, four, row_e, row_o, col_0, col_1, col_2,
     out_one, out_two, out_three, out_four, tile_a, tile_b,
 ):
     bands, n, m = shape
     above, below = from_rows(row_e, row_o)
-    even = (lax.axis_index("col") & 1) == 0
-    before = jnp.where(even, col_o[...], col_e[...])
-    after = jnp.where(even, col_e[...], col_o[...])
+    turn = lax.axis_index("col") % 3
+    got = [col_0[...], col_1[...], col_2[...]]
+    after = jnp.where(turn == 0, got[0], jnp.where(turn == 1, got[1], got[2]))
+    before = jnp.where(turn == 0, got[2], jnp.where(turn == 1, got[0], got[1]))
     fields, outs = [one, two, three, four], [out_one, out_two, out_three, out_four]
     tile_a[...] = jnp.zeros_like(tile_a)
     tile_b[...] = jnp.zeros_like(tile_b)
@@ -370,18 +387,20 @@
             start += lanes_of(cols)
 
 
-def swap(pair, axis, counts):
+def swap(values, axis, counts):
     sizes = [counts[name] for name in ("row", "col")]
     along = ("row", "col").index(axis)
     out = []
-    for parity, value in enumerate(pair):
+    for k, value in enumerate(values):
         moves = []
         for i in range(sizes[0] * sizes[1]):
             place = list(divmod(i, sizes[1]))
-            step = 1 if place[along] % 2 == parity else -1
             target = list(place)
-            if 0 <= place[along] + step < sizes[along]:
-                target[along] += step
+            here = place[along]
+            if here % len(values) == k and here + 1 < sizes[along]:
+                target[along] += 1
+            elif (here - 1) % len(values) == k and here > 0:
+                target[along] -= 1
             elif (place[1 - along] ^ 1) < sizes[1 - along]:
                 target[1 - along] ^= 1
             else:
@@ -440,25 +459,25 @@
             name="pyramid",
         )(field, *mats)
         row_e, row_o = swap((send_e, send_o), "row", mesh.shape)
-        send_e, send_o = pl.pallas_call(
+        sends = pl.pallas_call(
             functools.partial(rim_kernel, shape, counts),
-            out_shape=[col_part, col_part],
+            out_shape=[col_part] * 3,
             in_specs=[VMEM] * 4,
-            out_specs=[VMEM] * 2,
+            out_specs=[VMEM] * 3,
             scratch_shapes=[pltpu.VMEM((bands, 128, 128), F32)] * 2,
             compiler_params=pltpu.CompilerParams(vmem_limit_bytes=4 << 20),
             name="rim",
         )(rim_a, rim_b, row_e, row_o)
-        col_e, col_o = swap((send_e, send_o), "col", mesh.shape)
+        cols = swap(sends, "col", mesh.shape)
         return tuple(pl.pallas_call(
             functools.partial(finish_kernel, shape),
             out_shape=levels,
-            in_specs=[VMEM] * 8,
+            in_specs=[VMEM] * 9,
             out_specs=[VMEM] * 4,
             scratch_shapes=[pltpu.VMEM((bands, 128, 128), F32)] * 2,
             compiler_params=pltpu.CompilerParams(vmem_limit_bytes=8 << 20),
             name="finish",
-        )(*own, row_e, row_o, col_e, col_o))
+        )(*own, row_e, row_o, *cols))
 
     placed = P(None, "row", "col")
     return jax.shard_map(

time: 14.4 us -> 13.7 us (0.951)
  the two profiles are of different devices: /device:TPU:20 before, /device:TPU:0 now
where the time goes in v4:
time: 13.7 us; the launch traced here: 13.5 us
  Pallas kernels  5.91 us (43%)
  starting transfers between devices  5.48 us (40%)
  waiting for transfers between devices  1.45 us (11%)
  between operations  0.67 us (5%)
    ppermute x5, starting transfers between devices, swap(): out.append(lax.ppermute(value, ('row', 'col'), moves))  5.48 us
    pallas_call x1, Pallas kernels, local(): pl.pallas_call(functools.partial(pyramid_kernel, shape, counts), out_shap...  2.3 us
    pallas_call x1, Pallas kernels, local(): pl.pallas_call(functools.partial(edge_kernel, shape, counts), out_shape=[...  2.23 us
    ppermute x5, waiting for transfers between devices, swap(): out.append(lax.ppermute(value, ('row', 'col'), moves))  1.45 us
    pallas_call x1, Pallas kernels, local(): pl.pallas_call(functools.partial(finish_kernel, shape), out_shape=levels,...  1.17 us
  transfers between devices with their start and end apart: 5, of which 1 were waited for; matrix products, arithmetic and copies ran while one was open for 0% of the time, Pallas kernels for 17%

profile of v4, /device:TPU:0, one launch (start us, length us, event | category | flops | bytes accessed | tf_op | source)
XLA Modules:
  0.0 13.5 jit_solution(6560143147608233942)
XLA Ops:
  0.6 2.2 %edge.1 = (f32[8,1408]{1,0:T(8,128)S(1)}, f32[8,1408]{1,0:T(8,128)S(1)}, f32[3,8,288,128]{3,2,1,0:T(8,128)S(1)}, bf16[4,256,256]{2,1,0:T(8,128)(2,1)S(1)}, bf16[...) custom-call(f32[3,256,1024]{2,1,0:T(8,128)} %x_hbm.1), custom_call_target="tpu_custom_call" | custom-call | tf_op jit(solution)/shard_map/edge/pallas_call | solution.py:427
  2.9 0.5 %collective-permute-start = (f32[8,1408]{1,0:T(8,128)S(1)}, f32[8,1408]{1,0:T(8,128)S(1)}, u32[]{:S(2)}, u32[]{:S(2)}) collective-permute-start(f32[8,1408]{1,0:T(8,128)S(1)} %get-tuple-element.27), channel_id=1, source_target_pairs={{0,4},{1,5},{2,6},{3,7},{4,0},{5,1},{6,2},{7,3},{8,12},{9,13},{10,... | collective-permute-start | bytes 135176 | tf_op jit(solution)/shard_map/ppermute | solution.py:409
  3.4 2.7 %collective-permute-start.1 = (f32[8,1408]{1,0:T(8,128)S(1)}, f32[8,1408]{1,0:T(8,128)S(1)}, u32[]{:S(2)}, u32[]{:S(2)}) collective-permute-start(f32[8,1408]{1,0:T(8,128)S(1)} %get-tuple-element.28), channel_id=1, source_target_pairs={{0,1},{1,0},{2,3},{3,2},{4,8},{5,9},{6,10},{7,11},{8,4},{9,5},{10,... | collective-permute-start | bytes 135176 | tf_op jit(solution)/shard_map/ppermute | solution.py:409
  6.1 2.3 %pyramid.1 = (f32[3,128,512]{2,1,0:T(8,128)S(1)}, f32[3,64,256]{2,1,0:T(8,128)S(1)}, f32[3,32,128]{2,1,0:T(8,128)S(1)}, f32[3,16,64]{2,1,0:T(8,128)S(1)}, f32[3,...) custom-call(f32[3,8,288,128]{3,2,1,0:T(8,128)S(1)} %get-tuple-element.19.s0, ...), custom_call_target="tpu_custom_call" | custom-call | flops 8000000000 | tf_op jit(solution)/shard_map/pyramid/pallas_call | solution.py:451
  8.4 0.0 collective-permute-done.got_e.row_e
  8.4 0.0 collective-permute-done.1.got_o.row_o
  8.4 0.2 %rim.1 = (f32[16,128]{1,0:T(8,128)S(1)}, f32[16,128]{1,0:T(8,128)S(1)}, f32[16,128]{1,0:T(8,128)S(1)}) custom-call(f32[3,128,128]{2,1,0:T(8,128)S(1)} %get-tuple-element.29.rim_a, f32[3,128,128]{2,1,0:T(8,128)S(1)} %get-tuple-element.30.rim_b, f32[8,1408]{1,0:T(8,128)S(1)} %collective-permute-done.got_e.row_e, f32[8,1408]{1,0:T(8,128)S(1)} %collective-permute-done.1.got_o.row_o), custom_call_target="tpu_custom_call" | custom-call | tf_op jit(solution)/shard_map/rim/pallas_call | solution.py:462
  8.6 1.8 %collective-permute-start.2 = (f32[16,128]{1,0:T(8,128)S(1)}, f32[16,128]{1,0:T(8,128)S(1)}, u32[]{:S(2)}, u32[]{:S(2)}) collective-permute-start(f32[16,128]{1,0:T(8,128)S(1)} %get-tuple-element.31), channel_id=1, source_target_pairs={{0,1},{1,0},{2,6},{3,7},{4,5},{5,4},{6,2},{7,3},{8,9},{9,8},{10,14... | collective-permute-start | bytes 24584 | tf_op jit(solution)/shard_map/ppermute | solution.py:409
  10.4 0.0 collective-permute-start.3
  10.4 0.5 %collective-permute-start.4 = (f32[16,128]{1,0:T(8,128)S(1)}, f32[16,128]{1,0:T(8,128)S(1)}, u32[]{:S(2)}, u32[]{:S(2)}) collective-permute-start(f32[16,128]{1,0:T(8,128)S(1)} %get-tuple-element.33), channel_id=1, source_target_pairs={{0,4},{1,5},{2,3},{3,2},{4,0},{5,1},{6,7},{7,6},{8,12},{9,13},{10,... | collective-permute-start | bytes 24584 | tf_op jit(solution)/shard_map/ppermute | solution.py:409
  10.9 1.4 %collective-permute-done.2.col_0 = f32[16,128]{1,0:T(8,128)S(1)} collective-permute-done((f32[16,128]{1,0:T(8,128)S(1)}, f32[16,128]{1,0:T(8,128)S(1)}, u32[]{:S(2)}, u32[]{:S(2)}) %collective-permute-start.2) | collective-permute-done | bytes 8224 | tf_op jit(solution)/shard_map/ppermute | solution.py:409
  12.3 0.0 collective-permute-done.3.col_1
  12.3 0.0 collective-permute-done.4.col_2
  12.3 1.2 %finish.1 = (f32[3,128,512]{2,1,0:T(8,128)}, f32[3,64,256]{2,1,0:T(8,128)}, f32[3,32,128]{2,1,0:T(8,128)}, f32[3,16,64]{2,1,0:T(8,128)}) custom-call(f32[3,128,512]{2,1,0:T(8,128)S(1)} %get-tuple-element.23.one, f32[3,64,256]{2,1,0:T(8,128)S(1)} %get-tuple-element.24.two, f32[3,32,128]{2,1,0:T(8,128)S(1)} %get-tuple-element.25.three, ...), custom_call_target="tpu_custom_call" | custom-call | tf_op jit(solution)/shard_map/finish/pallas_call | solution.py:472
Async XLA Ops:
  2.9 5.5 %collective-permute-start = (f32[8,1408]{1,0:T(8,128)S(1)}, f32[8,1408]{1,0:T(8,128)S(1)}, u32[]{:S(2)}, u32[]{:S(2)}) collective-permute-start(f32[8,1408]{1,0:T(8,128)S(1)} %get-tuple-element.27), channel_id=1, source_target_pairs={{0,4},{1,5},{2,6},{3,7},{4,0},{5,1},{6,2},{7,3},{8,12},{9,13},{10,... | collective-permute-start | bytes 135176 | tf_op jit(solution)/shard_map/ppermute | solution.py:409
  3.4 5.0 %collective-permute-start.1 = (f32[8,1408]{1,0:T(8,128)S(1)}, f32[8,1408]{1,0:T(8,128)S(1)}, u32[]{:S(2)}, u32[]{:S(2)}) collective-permute-start(f32[8,1408]{1,0:T(8,128)S(1)} %get-tuple-element.28), channel_id=1, source_target_pairs={{0,1},{1,0},{2,3},{3,2},{4,8},{5,9},{6,10},{7,11},{8,4},{9,5},{10,... | collective-permute-start | bytes 135176 | tf_op jit(solution)/shard_map/ppermute | solution.py:409
  8.6 3.7 %collective-permute-start.2 = (f32[16,128]{1,0:T(8,128)S(1)}, f32[16,128]{1,0:T(8,128)S(1)}, u32[]{:S(2)}, u32[]{:S(2)}) collective-permute-start(f32[16,128]{1,0:T(8,128)S(1)} %get-tuple-element.31), channel_id=1, source_target_pairs={{0,1},{1,0},{2,6},{3,7},{4,5},{5,4},{6,2},{7,3},{8,9},{9,8},{10,14... | collective-permute-start | bytes 24584 | tf_op jit(solution)/shard_map/ppermute | solution.py:409
  10.4 1.9 %collective-permute-start.3 = (f32[16,128]{1,0:T(8,128)S(1)}, f32[16,128]{1,0:T(8,128)S(1)}, u32[]{:S(2)}, u32[]{:S(2)}) collective-permute-start(f32[16,128]{1,0:T(8,128)S(1)} %get-tuple-element.32), channel_id=1, source_target_pairs={{0,4},{1,2},{2,1},{3,7},{4,0},{5,6},{6,5},{7,3},{8,12},{9,10},{10,... | collective-permute-start | bytes 24584 | tf_op jit(solution)/shard_map/ppermute | solution.py:409
  10.4 1.9 %collective-permute-start.4 = (f32[16,128]{1,0:T(8,128)S(1)}, f32[16,128]{1,0:T(8,128)S(1)}, u32[]{:S(2)}, u32[]{:S(2)}) collective-permute-start(f32[16,128]{1,0:T(8,128)S(1)} %get-tuple-element.33), channel_id=1, source_target_pairs={{0,4},{1,5},{2,3},{3,2},{4,0},{5,1},{6,7},{7,6},{8,12},{9,13},{10,... | collective-permute-start | bytes 24584 | tf_op jit(solution)/shard_map/ppermute | solution.py:409

commit v5 on v4

--- a/solution.py
+++ b/solution.py
@@ -129,6 +129,23 @@
     @pl.when(last)
     def _():
         ref[:, PAD + extent:PAD + extent + 1, :] = ref[:, PAD + extent - 2:PAD + extent - 1, :]
+
+
+def slots(bands, m):
+    place, tiles = {}, 0
+    for k in range(2, LEVELS + 1):
+        for t in range(lanes_of(m >> k) // 128):
+            for b in range(bands):
+                place[k, t, b] = tiles, 2 * b
+            tiles += 1
+    free = [(j, r) for j in range(tiles) for r in range(2 * bands, 8)]
+    for t in range(lanes_of(m >> 1) // 128):
+        for b in range(bands):
+            if not free:
+                free = [(tiles, r) for r in range(8)]
+                tiles += 1
+            place[1, t, b] = free.pop(0)
+    return place, tiles
 
 
 HEAD, FOOT = 16, 32
@@ -174,7 +191,7 @@
     for b in range(bands):
         for t in range(m // 128):
             e0[t, 64 * b + 8:64 * b + 56, :] = raw[b, :, 128 * t:128 * t + 128]
-    lane0 = 0
+    place, _ = slots(bands, m)
     for k, ref in enumerate((e0, e1, e2, e3)):
         stride = strides[k]
         head, foot, size = ((4, 24, 16), (5, 17, 8), (5, 16, 8), (5, 16, 8))[k]
@@ -201,14 +218,14 @@
         held = 8 + size
         first, count = ((23, 1), (14, 2), (10, 2), (8, 2))[k]
         for t, tile in enumerate(tiles):
-            wide = pl.ds(lane0, 128)
             for b in range(bands):
                 if k < LEVELS - 1:
                     stride_after = strides[k + 1]
                     (e1, e2, e3)[k][t, stride_after * b + 8:stride_after * b + 8 + held, :] = tile[held * b:held * b + held]
-                down[2 * b:2 * b + count, wide] = tile[held * b + first:held * b + first + count]
-                up[2 * b:2 * b + 1, wide] = tile[held * b:held * b + 1]
-            lane0 += 128
+                spot, line = place[k + 1, t, b]
+                wide = pl.ds(128 * spot, 128)
+                down[line:line + count, wide] = tile[held * b + first:held * b + first + count]
+                up[line:line + 1, wide] = tile[held * b:held * b + 1]
     lower_part = jnp.where(bottom, 0.0, down[...])
     upper_part = jnp.where(top, 0.0, up[...])
     even = (row & 1) == 0
@@ -283,14 +300,13 @@
     return jnp.where(even, o, e), jnp.where(even, e, o)
 
 
-def upper(part, b):
-    part = pltpu.roll(part, 8 - 2 * b, 0) if b else part
-    return jnp.where(iota(part.shape, 0) < 2, part, 0.0)
-
-
-def lower(part, b):
-    part = pltpu.roll(part, 7 - 2 * b, 0)
-    return jnp.where(iota(part.shape, 0) == 7, part, 0.0)
+def row_parts(above, below, place, k, t, b):
+    spot, line = place[k, t, b]
+    head, foot = (part[:, 128 * spot:128 * spot + 128] for part in (above, below))
+    sub = iota(head.shape, 0)
+    head = pltpu.roll(head, 8 - line, 0) if line else head
+    foot = pltpu.roll(foot, 7 - line, 0) if line < 7 else foot
+    return jnp.where(sub < (1 if k == 1 else 2), head, 0.0), jnp.where(sub == 7, foot, 0.0)
 
 
 def segments(n):
@@ -306,17 +322,13 @@
 ):
     bands, n, m = shape
     above, below = from_rows(got_e, got_o)
-    offsets, start = [], 0
-    for k in range(1, LEVELS + 1):
-        cols = m >> k
-        offsets.append(start + (cols if cols >= 128 else 0))
-        start += lanes_of(cols)
-
-    def rim_of(part, k):
-        part = part[:, offsets[k - 1]:offsets[k - 1] + 128]
+    place, _ = slots(bands, m)
+
+    def rim_of(k, b):
+        parts = row_parts(above, below, place, k, (m >> k) // 128, b)
         if (m >> k) < 128:
-            part = jnp.where(iota(part.shape, 1) < 2, pltpu.roll(part, 128 - (m >> k), 1), part)
-        return part
+            parts = [jnp.where(iota(p.shape, 1) < 2, pltpu.roll(p, 128 - (m >> k), 1), p) for p in parts]
+        return parts
 
     sub = iota((16, 128), 0)
     to_right, to_left = jnp.zeros((16, 128), F32), jnp.zeros((16, 128), F32)
@@ -325,8 +337,9 @@
         tile_a[b] = rim_a[b]
         tile_b[b] = rim_b[b]
         for ref, k, first, size in [(tile_a, 1, 0, half)] + [(tile_b, k, s, z) for k, s, z in segments(n)]:
-            ref[b, first:first + 8, :] += upper(rim_of(above, k), b)
-            ref[b, first + size - 8:first + size, :] += lower(rim_of(below, k), b)
+            head, foot = rim_of(k, b)
+            ref[b, first:first + 8, :] += head
+            ref[b, first + size - 8:first + size, :] += foot
         a = jnp.transpose(tile_a[b])
         c = jnp.transpose(tile_b[b])
         to_right = jnp.where(sub == 4 * b, a[0:1], to_right)
@@ -342,49 +355,95 @@
         send[...] = jnp.where(col % 3 == k, to_right, left)
 
 
-def finish_kernel(
-    shape, one, two, three, four, row_e, row_o, col_0, col_1, col_2,
-    out_one, out_two, out_three, out_four, tile_a, tile_b,
+def settle_kernel(
+    shape, one, two, three, four, row_e, row_o, out, done_one, done_two, done_three, done_four, inner, sems
 ):
     bands, n, m = shape
     above, below = from_rows(row_e, row_o)
+    place, _ = slots(bands, m)
+    tiles = (m >> 1) // 128
+    copies = []
+    for b in range(bands):
+        for k, (field, done) in enumerate(zip((one, two, three, four), (done_one, done_two, done_three, done_four)), 1):
+            cols, size = m >> k, n >> k
+            wide = min(cols, 128)
+            for t in range(cols // wide):
+                at, to, ref = pl.ds(wide * t, wide), pl.ds(wide * t, wide), done
+                if k == 1:
+                    if 0 < t < tiles - 1:
+                        ref, to = inner, pl.ds(128 * (t - 1), 128)
+                    else:
+                        to = pl.ds(128 * min(t, 1), 128)
+                head, foot = row_parts(above, below, place, k, t, b)
+                ref[b, 0:8, to] = field[b, 0:8, at] + head[:, :wide]
+                if size > 16:
+                    ref[b, 8:size - 8, to] = field[b, 8:size - 8, at]
+                ref[b, size - 8:size, to] = field[b, size - 8:size, at] + foot[:, :wide]
+            if k == 1:
+                copy = pltpu.make_async_copy(
+                    inner.at[b], out.at[b, :, pl.ds(128, 128 * (tiles - 2))], sems.at[b]
+                )
+                copy.start()
+                copies.append(copy)
+    for copy in copies:
+        copy.wait()
+
+
+def finish_kernel(
+    shape, _, one, two, three, four, col_0, col_1, col_2,
+    out_one, out_two, out_three, out_four, tile_a, tile_b, new_one, new_two, new_three, new_four, sems,
+):
+    bands, n, m = shape
     turn = lax.axis_index("col") % 3
     got = [col_0[...], col_1[...], col_2[...]]
     after = jnp.where(turn == 0, got[0], jnp.where(turn == 1, got[1], got[2]))
     before = jnp.where(turn == 0, got[2], jnp.where(turn == 1, got[0], got[1]))
-    fields, outs = [one, two, three, four], [out_one, out_two, out_three, out_four]
+    fields, news = [one, two, three, four], [new_one, new_two, new_three, new_four]
+    outs = [out_one, out_two, out_three, out_four]
     tile_a[...] = jnp.zeros_like(tile_a)
     tile_b[...] = jnp.zeros_like(tile_b)
     lane = iota((128, 128), 1)
+    copies = []
+
+    def send(source, target):
+        copy = pltpu.make_async_copy(source, target, sems.at[len(copies)])
+        copy.start()
+        copies.append(copy)
+
+    def add(k, b, part):
+        cols, size = m >> k, part.shape[0]
+        wide = min(cols, 128)
+        spot = lane[:size, :wide]
+        part = part[:, :wide]
+        low, high = jnp.where(spot < 2, part, 0.0), jnp.where(spot == wide - 1, part, 0.0)
+        count = min(cols // wide, 2)
+        for t in range(count):
+            at = pl.ds(wide * t, wide)
+            value = fields[k - 1][b, :, at]
+            if t == 0:
+                value = value + low
+            if t == count - 1:
+                value = value + high
+            news[k - 1][b, :, at] = value
+
     for b in range(bands):
         tile_a[b, 0:1, :] = before[4 * b:4 * b + 1]
         tile_a[b, 127:128, :] = after[4 * b:4 * b + 1]
         tile_b[b, 0:2, :] = before[4 * b + 1:4 * b + 3]
         tile_b[b, 127:128, :] = after[4 * b + 1:4 * b + 2]
         tile_b[b, 63:64, :] = after[4 * b + 1:4 * b + 2]
-        a = jnp.transpose(tile_a[b])
+    for b in range(bands):
+        add(1, b, jnp.transpose(tile_a[b]))
+        for t, at in enumerate((0, (m >> 1) - 128)):
+            send(new_one.at[b, :, pl.ds(128 * t, 128)], out_one.at[b, :, pl.ds(at, 128)])
+    for b in range(bands):
         c = jnp.transpose(tile_b[b])
-        start = 0
-        for k, first, size in [(1, 0, n // 2)] + segments(n):
-            cols = m >> k
-            part = (a if k == 1 else c)[first:first + size]
-            wide = min(cols, 128)
-            spot = lane[:size, :wide]
-            part = part[:, :wide]
-            low, high = jnp.where(spot < 2, part, 0.0), jnp.where(spot == wide - 1, part, 0.0)
-            for t in range(cols // wide):
-                at = pl.ds(wide * t, wide)
-                value = fields[k - 1][b, :, at]
-                if t == 0:
-                    value = value + low
-                if t == cols // wide - 1:
-                    value = value + high
-                outs[k - 1][b, :, at] = value
-            top = upper(above[:, start:start + cols], b)
-            end = lower(below[:, start:start + cols], b)
-            outs[k - 1][b, 0:8, :] += top
-            outs[k - 1][b, size - 8:size, :] += end
-            start += lanes_of(cols)
+        for k, first, size in segments(n):
+            add(k, b, c[first:first + size])
+    for new, out in zip(news[1:], outs[1:]):
+        send(new, out)
+    for copy in copies:
+        copy.wait()
 
 
 def swap(values, axis, counts):
@@ -416,7 +475,7 @@
     def local(relief):
         shape = bands, n, m = relief.shape
         levels = [jax.ShapeDtypeStruct((bands, n >> k, m >> k), F32) for k in range(1, LEVELS + 1)]
-        width = sum(lanes_of(m >> k) for k in range(1, LEVELS + 1))
+        width = 128 * slots(bands, m)[1]
         row_part = jax.ShapeDtypeStruct((8, width), F32)
         col_part = jax.ShapeDtypeStruct((16, 128), F32)
         rim = jax.ShapeDtypeStruct((bands, 128, 128), F32)
@@ -469,15 +528,32 @@
             name="rim",
         )(rim_a, rim_b, row_e, row_o)
         cols = swap(sends, "col", mesh.shape)
+        ends = jax.ShapeDtypeStruct((bands, n >> 1, 256), F32)
+        hbm = pl.BlockSpec(memory_space=pltpu.HBM)
+        out, *done = pl.pallas_call(
+            functools.partial(settle_kernel, shape),
+            out_shape=[levels[0], ends] + levels[1:],
+            in_specs=[VMEM] * 6,
+            out_specs=[hbm] + [VMEM] * 4,
+            scratch_shapes=[
+                pltpu.VMEM((bands, n >> 1, (m >> 1) - 256), F32), pltpu.SemaphoreType.DMA((bands,)),
+            ],
+            compiler_params=pltpu.CompilerParams(vmem_limit_bytes=8 << 20),
+            cost_estimate=pl.CostEstimate(flops=2_000_000_000, bytes_accessed=0, transcendentals=0),
+            name="settle",
+        )(*own, row_e, row_o)
         return tuple(pl.pallas_call(
             functools.partial(finish_kernel, shape),
             out_shape=levels,
-            in_specs=[VMEM] * 9,
-            out_specs=[VMEM] * 4,
-            scratch_shapes=[pltpu.VMEM((bands, 128, 128), F32)] * 2,
+            in_specs=[hbm] + [VMEM] * 7,
+            out_specs=[hbm] * 4,
+            scratch_shapes=[pltpu.VMEM((bands, 128, 128), F32)] * 2 + [
+                pltpu.VMEM(level.shape, F32) for level in [ends] + levels[1:]
+            ] + [pltpu.SemaphoreType.DMA((2 * bands + LEVELS - 1,))],
+            input_output_aliases={0: 0},
             compiler_params=pltpu.CompilerParams(vmem_limit_bytes=8 << 20),
             name="finish",
-        )(*own, row_e, row_o, *cols))
+        )(out, *done, *cols))
 
     placed = P(None, "row", "col")
     return jax.shard_map(

time: 13.7 us -> 13.5 us (0.985)
  Pallas kernels: 5.91 us -> 6.53 us
  waiting for transfers between devices: 1.45 us -> 0.83 us
  starting transfers between devices: 5.48 us -> 5.3 us
    pallas_call x0 -> x1, Pallas kernels: none -> 0.79 us  [local(): pl.pallas_call(functools.partial(settle_kernel, shape), out_shape=[levels...]
    ppermute x5, waiting for transfers between devices: 1.45 us -> 0.83 us  [swap(): out.append(lax.ppermute(value, ('row', 'col'), moves))]
    ppermute x5, starting transfers between devices: 5.48 us -> 5.3 us  [swap(): out.append(lax.ppermute(value, ('row', 'col'), moves))]
    pallas_call x1, Pallas kernels: 1.17 us -> 1.02 us  [local(): pl.pallas_call(functools.partial(finish_kernel, shape), out_shape=levels,...]
  transfers between devices with their start and end apart: 5 -> 5, of which waited for: 1 -> 1; matrix products, arithmetic and copies ran while one was open for 0% -> 0% of each run, Pallas kernels for 17% -> 23%
where the time goes in v5:
time: 13.5 us; the launch traced here: 13.3 us
  Pallas kernels  6.53 us (48%)
  starting transfers between devices  5.3 us (39%)
  waiting for transfers between devices  0.83 us (6%)
  between operations  0.67 us (5%)
    ppermute x5, starting transfers between devices, swap(): out.append(lax.ppermute(value, ('row', 'col'), moves))  5.3 us
    pallas_call x1, Pallas kernels, local(): pl.pallas_call(functools.partial(pyramid_kernel, shape, counts), out_shap...  2.3 us
    pallas_call x1, Pallas kernels, local(): pl.pallas_call(functools.partial(edge_kernel, shape, counts), out_shape=[...  2.23 us
    pallas_call x1, Pallas kernels, local(): pl.pallas_call(functools.partial(finish_kernel, shape), out_shape=levels,...  1.02 us
    ppermute x5, waiting for transfers between devices, swap(): out.append(lax.ppermute(value, ('row', 'col'), moves))  0.83 us
    pallas_call x1, Pallas kernels, local(): pl.pallas_call(functools.partial(settle_kernel, shape), out_shape=[levels...  0.79 us
  transfers between devices with their start and end apart: 5, of which 1 were waited for; matrix products, arithmetic and copies ran while one was open for 0% of the time, Pallas kernels for 23%

profile of v5, /device:TPU:0, one launch (start us, length us, event | category | flops | bytes accessed | tf_op | source)
XLA Modules:
  0.0 13.3 jit_solution(12930271010718180334)
XLA Ops:
  0.6 2.2 %edge.1 = (f32[8,896]{1,0:T(8,128)S(1)}, f32[8,896]{1,0:T(8,128)S(1)}, f32[3,8,288,128]{3,2,1,0:T(8,128)S(1)}, bf16[4,256,256]{2,1,0:T(8,128)(2,1)S(1)}, bf16[12...) custom-call(f32[3,256,1024]{2,1,0:T(8,128)} %x_hbm.1), custom_call_target="tpu_custom_call" | custom-call | tf_op jit(solution)/shard_map/edge/pallas_call | solution.py:486
  2.9 0.5 %collective-permute-start = (f32[8,896]{1,0:T(8,128)S(1)}, f32[8,896]{1,0:T(8,128)S(1)}, u32[]{:S(2)}, u32[]{:S(2)}) collective-permute-start(f32[8,896]{1,0:T(8,128)S(1)} %get-tuple-element.32), channel_id=1, source_target_pairs={{0,4},{1,5},{2,6},{3,7},{4,0},{5,1},{6,2},{7,3},{8,12},{9,13},{10,... | collective-permute-start | bytes 86024 | tf_op jit(solution)/shard_map/ppermute | solution.py:468
  3.4 2.7 %collective-permute-start.1 = (f32[8,896]{1,0:T(8,128)S(1)}, f32[8,896]{1,0:T(8,128)S(1)}, u32[]{:S(2)}, u32[]{:S(2)}) collective-permute-start(f32[8,896]{1,0:T(8,128)S(1)} %get-tuple-element.33), channel_id=1, source_target_pairs={{0,1},{1,0},{2,3},{3,2},{4,8},{5,9},{6,10},{7,11},{8,4},{9,5},{10,... | collective-permute-start | bytes 86024 | tf_op jit(solution)/shard_map/ppermute | solution.py:468
  6.1 2.3 %pyramid.1 = (f32[3,128,512]{2,1,0:T(8,128)S(1)}, f32[3,64,256]{2,1,0:T(8,128)S(1)}, f32[3,32,128]{2,1,0:T(8,128)S(1)}, f32[3,16,64]{2,1,0:T(8,128)S(1)}, f32[3,...) custom-call(f32[3,8,288,128]{3,2,1,0:T(8,128)S(1)} %get-tuple-element.24.s0, ...), custom_call_target="tpu_custom_call" | custom-call | flops 8000000000 | tf_op jit(solution)/shard_map/pyramid/pallas_call | solution.py:510
  8.4 0.0 collective-permute-done.row_e.got_e
  8.4 0.0 collective-permute-done.1.row_o.got_o
  8.4 0.2 %rim.1 = (f32[16,128]{1,0:T(8,128)S(1)}, f32[16,128]{1,0:T(8,128)S(1)}, f32[16,128]{1,0:T(8,128)S(1)}) custom-call(f32[3,128,128]{2,1,0:T(8,128)S(1)} %get-tuple-element.39.rim_a, f32[3,128,128]{2,1,0:T(8,128)S(1)} %get-tuple-element.40.rim_b, f32[8,896]{1,0:T(8,128)S(1)} %collective-permute-done.row_e.got_e, f32[8,896]{1,0:T(8,128)S(1)} %collective-permute-done.1.row_o.got_o), custom_call_target="tpu_custom_call" | custom-call | tf_op jit(solution)/shard_map/rim/pallas_call | solution.py:521
  8.6 1.6 %collective-permute-start.2 = (f32[16,128]{1,0:T(8,128)S(1)}, f32[16,128]{1,0:T(8,128)S(1)}, u32[]{:S(2)}, u32[]{:S(2)}) collective-permute-start(f32[16,128]{1,0:T(8,128)S(1)} %get-tuple-element.41), channel_id=1, source_target_pairs={{0,1},{1,0},{2,6},{3,7},{4,5},{5,4},{6,2},{7,3},{8,9},{9,8},{10,14... | collective-permute-start | bytes 24584 | tf_op jit(solution)/shard_map/ppermute | solution.py:468
  10.2 0.0 collective-permute-start.3
  10.2 0.5 %collective-permute-start.4 = (f32[16,128]{1,0:T(8,128)S(1)}, f32[16,128]{1,0:T(8,128)S(1)}, u32[]{:S(2)}, u32[]{:S(2)}) collective-permute-start(f32[16,128]{1,0:T(8,128)S(1)} %get-tuple-element.43), channel_id=1, source_target_pairs={{0,4},{1,5},{2,3},{3,2},{4,0},{5,1},{6,7},{7,6},{8,12},{9,13},{10,... | collective-permute-start | bytes 24584 | tf_op jit(solution)/shard_map/ppermute | solution.py:468
  10.7 0.8 %settle.1 = (f32[3,128,512]{2,1,0:T(8,128)}, f32[3,128,256]{2,1,0:T(8,128)S(1)}, f32[3,64,256]{2,1,0:T(8,128)S(1)}, f32[3,32,128]{2,1,0:T(8,128)S(1)}, f32[3,16,64]{2,1,0:T(8,128)S(1)}) custom-call(f32[3,128,512]{2,1,0:T(8,128)S(1)} %get-tuple-element.28.one, f32[3,64,256]{2,1,0:T(8,128)S(1)} %get-tuple-element.29.two, ...), custom_call_target="tpu_custom_call" | custom-call | flops 2000000000 | tf_op jit(solution)/shard_map/settle/pallas_call | solution.py:533
  11.5 0.8 %collective-permute-done.2.col_0 = f32[16,128]{1,0:T(8,128)S(1)} collective-permute-done((f32[16,128]{1,0:T(8,128)S(1)}, f32[16,128]{1,0:T(8,128)S(1)}, u32[]{:S(2)}, u32[]{:S(2)}) %collective-permute-start.2) | collective-permute-done | bytes 8224 | tf_op jit(solution)/shard_map/ppermute | solution.py:468
  12.3 0.0 collective-permute-done.3.col_1
  12.3 0.0 collective-permute-done.4.col_2
  12.3 1.0 %finish.1 = (f32[3,128,512]{2,1,0:T(8,128)}, f32[3,64,256]{2,1,0:T(8,128)}, f32[3,32,128]{2,1,0:T(8,128)}, f32[3,16,64]{2,1,0:T(8,128)}) custom-call(f32[3,128,512]{2,1,0:T(8,128)} %get-tuple-element.34._, f32[3,128,256]{2,1,0:T(8,128)S(1)} %get-tuple-element.35.one, f32[3,64,256]{2,1,0:T(8,128)S(1)} %get-tuple-element.36.two, ...), custom_call_target="tpu_custom_call", output_to_operand_aliasing={{0}: (0, {})} | custom-call | tf_op jit(solution)/shard_map/finish/pallas_call | solution.py:545
Async XLA Ops:
  2.9 5.5 %collective-permute-start = (f32[8,896]{1,0:T(8,128)S(1)}, f32[8,896]{1,0:T(8,128)S(1)}, u32[]{:S(2)}, u32[]{:S(2)}) collective-permute-start(f32[8,896]{1,0:T(8,128)S(1)} %get-tuple-element.32), channel_id=1, source_target_pairs={{0,4},{1,5},{2,6},{3,7},{4,0},{5,1},{6,2},{7,3},{8,12},{9,13},{10,... | collective-permute-start | bytes 86024 | tf_op jit(solution)/shard_map/ppermute | solution.py:468
  3.4 5.0 %collective-permute-start.1 = (f32[8,896]{1,0:T(8,128)S(1)}, f32[8,896]{1,0:T(8,128)S(1)}, u32[]{:S(2)}, u32[]{:S(2)}) collective-permute-start(f32[8,896]{1,0:T(8,128)S(1)} %get-tuple-element.33), channel_id=1, source_target_pairs={{0,1},{1,0},{2,3},{3,2},{4,8},{5,9},{6,10},{7,11},{8,4},{9,5},{10,... | collective-permute-start | bytes 86024 | tf_op jit(solution)/shard_map/ppermute | solution.py:468
  8.6 3.7 %collective-permute-start.2 = (f32[16,128]{1,0:T(8,128)S(1)}, f32[16,128]{1,0:T(8,128)S(1)}, u32[]{:S(2)}, u32[]{:S(2)}) collective-permute-start(f32[16,128]{1,0:T(8,128)S(1)} %get-tuple-element.41), channel_id=1, source_target_pairs={{0,1},{1,0},{2,6},{3,7},{4,5},{5,4},{6,2},{7,3},{8,9},{9,8},{10,14... | collective-permute-start | bytes 24584 | tf_op jit(solution)/shard_map/ppermute | solution.py:468
  10.2 2.1 %collective-permute-start.3 = (f32[16,128]{1,0:T(8,128)S(1)}, f32[16,128]{1,0:T(8,128)S(1)}, u32[]{:S(2)}, u32[]{:S(2)}) collective-permute-start(f32[16,128]{1,0:T(8,128)S(1)} %get-tuple-element.42), channel_id=1, source_target_pairs={{0,4},{1,2},{2,1},{3,7},{4,0},{5,6},{6,5},{7,3},{8,12},{9,10},{10,... | collective-permute-start | bytes 24584 | tf_op jit(solution)/shard_map/ppermute | solution.py:468
  10.2 2.1 %collective-permute-start.4 = (f32[16,128]{1,0:T(8,128)S(1)}, f32[16,128]{1,0:T(8,128)S(1)}, u32[]{:S(2)}, u32[]{:S(2)}) collective-permute-start(f32[16,128]{1,0:T(8,128)S(1)} %get-tuple-element.43), channel_id=1, source_target_pairs={{0,4},{1,5},{2,3},{3,2},{4,0},{5,1},{6,7},{7,6},{8,12},{9,13},{10,... | collective-permute-start | bytes 24584 | tf_op jit(solution)/shard_map/ppermute | solution.py:468
